TPU v7x, 512 devices: a whole 4x4x16 slice. The times are simulated.
512 devices in a mesh: prow: 16 (over z), pcol: 32 (over x, y, core).
Axes of the slice: x: 4, y: 4, z: 16, core: 2. Of those that a mesh axis runs over, the one named last changes fastest.
Arguments:
- matrix: float32 [8192, 32768], P('prow', 'pcol'), may hold values from -6 to 6
- pivot_inverse: float32 [2, 512, 512], P(None, 'prow'), may hold values from -0.01171875 to 0.01171875
- row_live: int32 [2, 16], replicated, may hold values 0 or 1
- col_live: int32 [2, 64], replicated, may hold values 0 or 1
Outputs:
- factored: float32 [8192, 32768], P('prow', 'pcol')
All inputs are finite; a program needn't handle non-finite values.
Results may differ from a plain program's by a relative error of at most 0.0001.
Values sent between devices are 32-bit elements; how exact they have to be, the bound alone decides.
No kernel may reach another device: no remote copies, remote signals or barrier semaphores. Data moves between devices by JAX's collectives and lax.ppermute only.
A program may use at most 64 MiB of HBM per device.

v0:
```python
import jax
import jax.numpy as jnp
from jax import lax
from jax.sharding import PartitionSpec as P


def copy_for_each(value, axis):
    copies = jnp.broadcast_to(value, (lax.axis_size(axis), *value.shape))
    return lax.all_to_all(copies, axis, split_axis=0, concat_axis=0, tiled=True)


def laid_out(tiles, dim):
    tiles = jnp.moveaxis(tiles, 0, dim)
    dims = tiles.shape
    return tiles.reshape(*dims[:dim], dims[dim] * dims[dim + 1], *dims[dim + 2 :])


def gathered_copies(value, axis, dim):
    tiles = copy_for_each(value, axis)
    return laid_out(tiles, dim)


def spread(value, axis, source):
    kept = jnp.where(lax.axis_index(axis) == source, value, 0).astype(value.dtype)
    return lax.psum(kept, axis)


def filled_up(lines, length):
    spare = -lines.shape[0] % length
    if not spare:
        return lines
    return jnp.concatenate([lines, jnp.zeros((spare, *lines.shape[1:]), lines.dtype)])


def broadcast_by_parts(value, axis, root):
    lines = jnp.where(lax.axis_index(axis) == root, value, jnp.zeros_like(value)).reshape(
        -1, *value.shape[1:][-1:]
    )
    padded = filled_up(lines, lax.axis_size(axis))
    own = lax.psum_scatter(padded, axis, scatter_dimension=0, tiled=True)
    return lax.all_gather(own, axis, axis=0, tiled=True)[: len(lines)].reshape(value.shape)


def apply_pivot(column_part, pivot_rows):
    return jnp.einsum(
        "rbc,cd->rbd",
        column_part,
        gathered_copies(pivot_rows, "prow", 0),
        precision=lax.Precision.HIGHEST,
    )


def per_device(matrix, pivot_inverse, row_live, col_live):
    block_width = pivot_inverse.shape[2]
    row_blocks = matrix.shape[0] // block_width
    col_blocks = matrix.shape[1] // block_width
    pcol_here = lax.axis_index("pcol")
    row_index = jnp.arange(row_blocks, dtype=jnp.int32) * lax.axis_size("prow") + lax.axis_index(
        "prow"
    )
    col_index = jnp.arange(col_blocks, dtype=jnp.int32) * lax.axis_size("pcol") + pcol_here
    blocks = matrix.reshape(row_blocks, block_width, col_blocks, block_width)

    def lower_panel(column_part, panel):
        row_mask = jnp.where(row_index > panel, jnp.take(row_live[panel], row_index), 0).astype(
            jnp.float32
        )[:, None, None]
        received = spread(column_part, "pcol", panel)
        return apply_pivot(received, pivot_inverse[panel]) * row_mask

    def upper_row(current, panel):
        col_mask = jnp.where(col_index > panel, jnp.take(col_live[panel], col_index), 0).astype(
            jnp.float32
        )
        return broadcast_by_parts(current[0] * col_mask[None, :, None], "prow", panel)

    def store_lower(column_part, lower_part, panel):
        keep_rows = (row_index > panel)[:, None, None] & (pcol_here == panel)
        return jnp.where(keep_rows, lower_part, column_part)

    def outer_update(current, lower_part, upper_part):
        return current - jnp.einsum(
            "rbc,cjd->rbjd", lower_part, upper_part, precision=lax.Precision.HIGHEST
        )

    lower_part = lower_panel(blocks[:, :, 0, :], 0)
    upper_part = upper_row(blocks, 0)
    blocks = outer_update(blocks, lower_part, upper_part)
    blocks = blocks.at[:, :, 0, :].set(store_lower(blocks[:, :, 0, :], lower_part, 0))
    next_lower = lower_panel(blocks[:, :, 0, :], 1)
    next_upper = upper_row(blocks, 1)
    blocks = outer_update(blocks, next_lower, next_upper)
    blocks = blocks.at[:, :, 0, :].set(store_lower(blocks[:, :, 0, :], next_lower, 1))
    return blocks.reshape(row_blocks * block_width, col_blocks * block_width)


def solution(mesh):
    in_specs = (P("prow", "pcol"), P(None, "prow", None), P(), P())
    out_specs = P("prow", "pcol")
    return jax.shard_map(
        per_device, mesh=mesh, in_specs=in_specs, out_specs=out_specs, check_vma=False
    )
```

profile of v0, /device:TPU:6, one launch (start us, length us, event | category | flops | bytes accessed | tf_op | source)
XLA Modules:
  0.0 403.2 jit_solution(14999764444500926546)
XLA Ops:
  9.6 1.7 squeeze_reshape.3
  11.4 1.5 multiply_select_fusion.1
  13.0 1.5 copy-done
  14.5 2.8 reshape.162
  17.3 2.5 broadcast_select_fusion
  19.8 1.1 copy.28
  20.9 1.1 broadcast_in_dim.55
  22.0 15.2 %all-to-all-start = ((f32[16,32,512]{2,1,0:T(8,128)}), f32[16,32,512]{2,1,0:T(8,128)S(1)}, u32[]{:S(2)}, u32[]{:S(2)}) async-start(f32[16,32,512]{2,1,0:T(8,128)} %broadcast_in_dim.55), calls=%async_computation | async-start | bytes 2097152 | tf_op jit(solution)/shard_map/all_to_all | solution.py:9
  37.2 85.9 %reduce-scatter.3.cloned.1.call-done = f32[64,512]{1,0:T(8,128)} async-done(((f32[1024,512]{1,0:T(8,128)}), f32[64,512]{1,0:T(8,128)}) %reduce-scatter.3.cloned.1.call-update) | async-done | bytes 131088 | tf_op jit(solution)/shard_map/reduce_scatter | solution.py:40
  123.4 1.8 copy.7
  126.5 2.9 copy.9
  129.5 33.5 %all-reduce.3.cloned.1.call-done = f32[512,512]{1,0:T(8,128)} async-done(((f32[512,512]{1,0:T(8,128)}), f32[512,512]{1,0:T(8,128)}) %all-reduce.3.cloned.1.call-update) | async-done | bytes 1048592 | tf_op jit(solution)/shard_map/psum | solution.py:25
  163.0 1.0 copy-done.1
  164.0 3.4 convolution_multiply_fusion.1
  167.4 28.6 %all-gather.3.cloned.1.call-done = f32[1024,512]{1,0:T(8,128)} async-done(((f32[64,512]{1,0:T(8,128)}), f32[1024,512]{1,0:T(8,128)}) %all-gather.3.cloned.1.call-update) | async-done | bytes 2097168 | tf_op jit(solution)/shard_map/all_gather | solution.py:41
  196.0 3.4 reshape.165
  199.5 5.9 %subtract_bitcast_fusion = f32[1,512,2,512]{3,1,2,0:T(8,128)S(1)} fusion(f32[512,2,512]{2,0,1:T(8,128)} %copy.9, f32[512,2,512]{2,1,0:T(2,128)} %reshape.165, f32[512,512]{1,0:T(8,128)S(1)} %convolution_multiply_fusion.1), kind=kOutput, calls=%fused_computation.8 | convolution fusion | flops 3221749760 | bytes 7340032 | tf_op jit(solution)/shard_map/rbc,cjd->rbjd/dot_general | solution.py:82
  205.4 1.2 broadcast_select_fusion.1
  206.7 2.9 copy.11
  209.6 3.7 squeeze.35
  213.3 3.1 multiply_select_fusion
  217.0 1.1 broadcast_in_dim.61
  218.1 7.6 %all-to-all-start.1 = ((f32[16,32,512]{2,1,0:T(8,128)}), f32[16,32,512]{2,1,0:T(8,128)S(1)}, u32[]{:S(2)}, u32[]{:S(2)}) async-start(f32[16,32,512]{2,1,0:T(8,128)} %broadcast_in_dim.61), calls=%async_computation.2 | async-start | bytes 2097152 | tf_op jit(solution)/shard_map/all_to_all | solution.py:9
  226.0 80.5 %reduce-scatter.5.cloned.1.call-done = f32[64,512]{1,0:T(8,128)} async-done(((f32[1024,512]{1,0:T(8,128)}), f32[64,512]{1,0:T(8,128)}) %reduce-scatter.5.cloned.1.call-update) | async-done | bytes 131088 | tf_op jit(solution)/shard_map/reduce_scatter | solution.py:40
  307.2 47.7 %all-reduce.5.cloned.1.call-done = f32[512,512]{1,0:T(8,128)} async-done(((f32[512,512]{1,0:T(8,128)}), f32[512,512]{1,0:T(8,128)}) %all-reduce.5.cloned.1.call-update) | async-done | bytes 1048592 | tf_op jit(solution)/shard_map/psum | solution.py:25
  354.9 3.4 convolution_multiply_fusion
  358.4 21.5 %all-gather.5.cloned.1.call-done = f32[1024,512]{1,0:T(8,128)} async-done(((f32[64,512]{1,0:T(8,128)}), f32[1024,512]{1,0:T(8,128)}) %all-gather.5.cloned.1.call-update) | async-done | bytes 2097168 | tf_op jit(solution)/shard_map/all_gather | solution.py:41
  379.9 3.4 reshape.168
  383.3 6.6 %bitcast_subtract_fusion = f32[1,512,2,512]{3,1,2,0:T(8,128)} fusion(f32[1,512,2,512]{3,1,2,0:T(8,128)S(1)} %bitcast_dynamic-update-slice_fusion, f32[512,2,512]{2,1,0:T(2,128)} %reshape.168, f32[512,512]{1,0:T(8,128)S(1)} %convolution_multiply_fusion), kind=kOutput, calls=%fused_computation.2 | convolution fusion | flops 3221749760 | bytes 7340032 | tf_op jit(solution)/shard_map/rbc,cjd->rbjd/dot_general | solution.py:82
  389.9 2.4 fusion.10
  392.3 1.9 copy.14
  394.3 1.8 copy.15
  (36 shorter events, 4.4 us)
Async XLA Ops:
  7.4 115.7 %reduce-scatter.3.cloned.1.call-start = ((), (), s32[]{:S(2)}) async-start(), calls=%async_computation.5 | async-start | bytes 2228224 | tf_op jit(solution)/shard_map/reduce_scatter | solution.py:40
  12.9 1.6 copy-start
  12.9 150.1 %all-reduce.3.cloned.1.call-start = ((), (), s32[]{:S(2)}) async-start(), calls=%async_computation.4 | async-start | bytes 2097152 | tf_op jit(solution)/shard_map/psum | solution.py:25
  19.8 1.1 copy-start.3
  22.0 141.0 %all-to-all-start = ((f32[16,32,512]{2,1,0:T(8,128)}), f32[16,32,512]{2,1,0:T(8,128)S(1)}, u32[]{:S(2)}, u32[]{:S(2)}) async-start(f32[16,32,512]{2,1,0:T(8,128)} %broadcast_in_dim.55), calls=%async_computation | async-start | bytes 2097152 | tf_op jit(solution)/shard_map/all_to_all | solution.py:9
  37.2 158.9 %all-gather.3.cloned.1.call-start = ((), (), s32[]{:S(2)}) async-start(), calls=%async_computation.6 | async-start | bytes 2228224 | tf_op jit(solution)/shard_map/all_gather | solution.py:41
  123.1 183.4 %reduce-scatter.5.cloned.1.call-start = ((), (), s32[]{:S(2)}) async-start(), calls=%async_computation.8 | async-start | bytes 2228224 | tf_op jit(solution)/shard_map/reduce_scatter | solution.py:40
  123.4 1.8 copy-start.4
  163.0 1.0 copy-start.1
  216.4 138.5 %all-reduce.5.cloned.1.call-start = ((), (), s32[]{:S(2)}) async-start(), calls=%async_computation.7 | async-start | bytes 2097152 | tf_op jit(solution)/shard_map/psum | solution.py:25
  218.1 89.1 %all-to-all-start.1 = ((f32[16,32,512]{2,1,0:T(8,128)}), f32[16,32,512]{2,1,0:T(8,128)S(1)}, u32[]{:S(2)}, u32[]{:S(2)}) async-start(f32[16,32,512]{2,1,0:T(8,128)} %broadcast_in_dim.61), calls=%async_computation.2 | async-start | bytes 2097152 | tf_op jit(solution)/shard_map/all_to_all | solution.py:9
  225.7 154.2 %all-gather.5.cloned.1.call-start = ((), (), s32[]{:S(2)}) async-start(), calls=%async_computation.9 | async-start | bytes 2228224 | tf_op jit(solution)/shard_map/all_gather | solution.py:41
  307.2 47.7 %copy-start.2 = (f32[16,32,512]{2,1,0:T(8,128)}, f32[16,32,512]{2,1,0:T(8,128)S(1)}, u32[]{:S(2)}) copy-start(f32[16,32,512]{2,1,0:T(8,128)S(1)} %all-to-all-done.1) | copy-start | bytes 3145732
Sparse Core Ops, SparseCore 0:
  13.1 109.9 reduce-scatter.2
  125.2 70.8 all-gather.2
  216.5 89.9 reduce-scatter.4
  308.5 71.3 all-gather.4
Sparse Core Ops, SparseCore 1:
  20.9 142.0 all-reduce.2
  220.1 134.8 all-reduce.4
where the time goes:
time: 404 us; the launch traced here: 403 us
  waiting for transfers between devices  298 us (74%)
  local copies, waits for them, and re-layouts  34.7 us (9%)
  starting transfers between devices  23.4 us (6%)
  matrix products  19.3 us (5%)
  between operations  16 us (4%)
  other arithmetic  11.4 us (3%)
    reduce_scatter x2, waiting for transfers between devices, broadcast_by_parts(): own = lax.psum_scatter(padded, axis, scatter_dimension=0, tiled=True)  166 us
    psum x2, waiting for transfers between devices, spread(): return lax.psum(kept, axis)  81.2 us
    all_gather x2, waiting for transfers between devices, broadcast_by_parts(): lax.all_gather(own, axis, axis=0, tiled=True)[:len(lines)]  50.2 us
    all_to_all x2, starting transfers between devices, copy_for_each(): return lax.all_to_all(copies, axis, split_axis=0, concat_axis=0, tiled=True)  22.8 us
    dot_general x2, matrix products, outer_update(): jnp.einsum('rbc,cjd->rbjd', lower_part, upper_part, precision=lax.Precisi...  12.5 us
  transfers between devices with their start and end apart: 8, of which 6 were waited for; matrix products, arithmetic and copies ran while one was open for 5% of the time, Pallas kernels for 0%

commit v1 on v0

v1 whole, which is shorter than its diff:
```python
import jax
import jax.numpy as jnp
from jax import lax
from jax.sharding import PartitionSpec as P


ROWS, COLS = "prow", "pcol"
TILE = 8


def matmul(a, b):
    return jnp.dot(a, b, precision=lax.Precision.HIGH)


def exchange(pieces, axis, groups=None):
    return lax.all_to_all(
        pieces, axis, split_axis=0, concat_axis=0, tiled=True, axis_index_groups=groups
    )


def copies(piece, count):
    return jnp.broadcast_to(piece, (count, *piece.shape))


def send_order(count):
    half = [d for i in range(1, count // 2) for d in (i, count - i)]
    return [count // 2, *reversed(half)]


def scatter_rows(matrix):
    count, here = lax.axis_size(ROWS), lax.axis_index(ROWS)
    length = matrix.shape[0] // count
    turned = jnp.where(here == 1, jnp.roll(matrix, -length, axis=0), matrix)
    first = second = turned[:length]
    for d in send_order(count):
        pairs = [(0, d), (1, (1 + d) % count)]
        came = lax.ppermute(turned[d * length : (d + 1) * length], ROWS, pairs)
        first = jnp.where(here == d, came, first)
        second = jnp.where(here == (1 + d) % count, came, second)
    return jnp.concatenate([first, second], axis=0)


def plane(count):
    side = round((count // 2) ** 0.5)
    return side, lambda x, y, core: (x * side + y) * 2 + core


def holders(blocks):
    count = blocks.shape[0]
    side, _ = plane(count)
    grid = blocks.reshape(2, side, side, *blocks.shape[1:])
    both = jnp.stack([jnp.swapaxes(grid[0], 0, 1), grid[1]], axis=2)
    return both.reshape(blocks.shape)


def gather_plane(piece):
    count, core = lax.axis_size(COLS), lax.axis_index(COLS) % 2
    side, at = plane(count)
    span = range(side)
    along_x = [[[at(x, y, c) for x in span] for y in span] for c in (0, 1)]
    along_y = [[[at(x, y, c) for y in span] for x in span] for c in (0, 1)]
    part = exchange(copies(piece, side), COLS, along_x[0] + along_y[1])
    part = exchange(copies(part, side), COLS, along_y[0] + along_x[1])
    part = part.reshape(side * side, *piece.shape)
    other = lax.ppermute(part, COLS, [(i, i ^ 1) for i in range(count)])
    low, high = jnp.where(core == 0, part, other), jnp.where(core == 0, other, part)
    return jnp.concatenate([low, high], axis=0)


def per_device(matrix, pivot_inverse, row_live, col_live):
    width = pivot_inverse.shape[2]
    n_rows, n_cols = lax.axis_size(ROWS), lax.axis_size(COLS)
    g, p = lax.axis_index(ROWS), lax.axis_index(COLS)
    lines = width // n_cols
    lane = width * 2 * pivot_inverse.shape[1] // (TILE * n_cols)
    row_groups, col_groups = pivot_inverse.shape[1] // TILE, width // lane

    spread = exchange(holders(matrix[:, :width].reshape(n_cols, lines, width)), COLS)
    mine = spread[:2]

    raw = lax.all_gather(scatter_rows(matrix), ROWS, axis=0, tiled=True)
    raw = raw.reshape(n_rows, 2, -1, matrix.shape[1])
    raw0, raw1 = raw[:, 0].reshape(matrix.shape), raw[:, 1].reshape(matrix.shape)

    sent = jnp.where(g == 0, mine[1], mine[0]).reshape(n_rows, lines // n_rows, width)
    got = exchange(sent, ROWS)[:2]
    tiles = pivot_inverse.reshape(2, row_groups, TILE, col_groups, lane)
    tiles = tiles.transpose(0, 1, 3, 2, 4).reshape(n_cols, TILE, lane)
    tile = lax.dynamic_index_in_dim(holders(tiles), p, keepdims=False)
    small = jnp.concatenate([got.reshape(-1, lane), tile], axis=0)
    split = got.size // lane
    small = exchange(copies(small, n_rows), ROWS)
    cross = small[:, :split].reshape(n_rows, 2, lines // n_rows, width)
    cross = cross.transpose(1, 0, 2, 3).reshape(2 * lines, width)
    wide = width // lane
    pivots = small[:, split:].reshape(n_rows // wide, wide, TILE, lane)
    pivots = pivots.transpose(0, 2, 1, 3).reshape(-1, width)

    piece = jnp.concatenate([mine.reshape(2 * lines, width), cross, pivots], axis=0)
    shared = gather_plane(piece)
    a_g0, a_g1, a_01, a_10 = (
        shared[:, i * lines : (i + 1) * lines].reshape(width, width) for i in range(4)
    )
    inverse = shared[:, 4 * lines :].reshape(
        2, row_groups, col_groups, n_rows // wide, TILE, wide, lane
    )
    inverse = inverse.transpose(0, 3, 5, 1, 4, 2, 6).reshape(2, width, width)

    def lower(panel, row):
        return jnp.where(row > panel, row_live[panel, row], 0).astype(jnp.float32)

    col_index = jnp.arange(matrix.shape[1] // width, dtype=jnp.int32) * n_cols + p

    def upper(panel):
        live = jnp.where(col_index > panel, jnp.take(col_live[panel], col_index), 0)
        return live.astype(jnp.float32)

    up0, up1 = upper(0), upper(1)
    both = matmul(jnp.concatenate([a_g0, a_10], axis=0), inverse[0])
    lower0 = both[:width] * lower(0, g)
    pivot_lower = both[width:] * lower(0, jnp.int32(1))
    a_g1 = a_g1 - matmul(lower0, a_01 * col_live[0, 1].astype(jnp.float32))
    lower1 = matmul(a_g1, inverse[1]) * lower(1, g)
    mixed = matmul(lower1, pivot_lower)

    out = []
    for j in range(matrix.shape[1] // width):
        span = slice(j * width, (j + 1) * width)
        left0 = (lower0 - mixed * up1[j]) * up0[j]
        block = matrix[:, span] - matmul(left0, raw0[:, span])
        block = block - matmul(lower1 * up1[j], raw1[:, span])
        if j == 0:
            block = jnp.where((p == 0) & (g > 0), lower0, block)
            block = jnp.where((p == 1) & (g > 1), lower1, block)
        out.append(block)
    return jnp.concatenate(out, axis=1)


def solution(mesh):
    in_specs = (P(ROWS, COLS), P(None, ROWS, None), P(), P())
    return jax.shard_map(
        per_device, mesh=mesh, in_specs=in_specs, out_specs=P(ROWS, COLS), check_vma=False
    )
```

time: 404 us -> 231 us (0.57)
  waiting for transfers between devices: 298 us -> 99.8 us
  starting transfers between devices: 23.4 us -> 66.3 us
  local copies, waits for them, and re-layouts: 34.7 us -> 23 us
  matrix products: 19.3 us -> 14.2 us
    reduce_scatter x2 -> x0, waiting for transfers between devices: 166 us -> none  [broadcast_by_parts(): own = lax.psum_scatter(padded, axis, scatter_dimension=0, tiled=True)]
    psum x2 -> x0, waiting for transfers between devices: 81.2 us -> none  [spread(): return lax.psum(kept, axis)]
    all_to_all x2 -> x5, waiting for transfers between devices: 0.01 us -> 54.2 us  [exchange(): lax.all_to_all(pieces, axis, split_axis=0, concat_axis=0, tiled=True, axi...]
    ppermute x0 -> x16, starting transfers between devices: none -> 30 us  [the longest x15 27.9 us: scatter_rows(): came = lax.ppermute(turned[d * length:(d + 1) * length], ROWS, pairs)]
    all_gather x2 -> x1, waiting for transfers between devices: 50.2 us -> 29.8 us  [per_device(): raw = lax.all_gather(scatter_rows(matrix), ROWS, axis=0, tiled=True)]
    ppermute x0 -> x16, waiting for transfers between devices: none -> 15.8 us  [the longest x15 15.8 us: scatter_rows(): came = lax.ppermute(turned[d * length:(d + 1) * length], ROWS, pairs)]
    reshape x5 -> x1, local copies, waits for them, and re-layouts: 14.4 us -> 0.04 us  [per_device(): cross = small[:, :split].reshape(n_rows, 2, lines // n_rows, width)]
    all_to_all x2 -> x5, starting transfers between devices: 22.8 us -> 36.3 us  [exchange(): lax.all_to_all(pieces, axis, split_axis=0, concat_axis=0, tiled=True, axi...]
  transfers between devices with their start and end apart: 8 -> 22, of which waited for: 6 -> 10; matrix products, arithmetic and copies ran while one was open for 5% -> 12% of each run, Pallas kernels for 0% -> 0%
where the time goes in v1:
time: 231 us; the launch traced here: 230 us
  waiting for transfers between devices  99.8 us (43%)
  starting transfers between devices  66.3 us (29%)
  local copies, waits for them, and re-layouts  23 us (10%)
  between operations  16.7 us (7%)
  matrix products  14.2 us (6%)
  other arithmetic  9.93 us (4%)
    all_to_all x5, waiting for transfers between devices, exchange(): lax.all_to_all(pieces, axis, split_axis=0, concat_axis=0, tiled=True, axi...  54.2 us
    all_to_all x5, starting transfers between devices, exchange(): lax.all_to_all(pieces, axis, split_axis=0, concat_axis=0, tiled=True, axi...  36.3 us
    all_gather x1, waiting for transfers between devices, per_device(): raw = lax.all_gather(scatter_rows(matrix), ROWS, axis=0, tiled=True)  29.8 us
    ppermute x15, starting transfers between devices, scatter_rows(): came = lax.ppermute(turned[d * length:(d + 1) * length], ROWS, pairs)  27.9 us
    ppermute x15, waiting for transfers between devices, scatter_rows(): came = lax.ppermute(turned[d * length:(d + 1) * length], ROWS, pairs)  15.8 us
    dot_general x8, matrix products, matmul(): return jnp.dot(a, b, precision=lax.Precision.HIGH)  14.2 us
    unnamed x18, local copies, waits for them, and re-layouts  5.28 us
  transfers between devices with their start and end apart: 22, of which 10 were waited for; matrix products, arithmetic and copies ran while one was open for 12% of the time, Pallas kernels for 0%

profile of v1, /device:TPU:6, one launch (start us, length us, event | category | flops | bytes accessed | tf_op | source)
XLA Modules:
  0.0 230.0 jit_solution(17562886922233837947)
XLA Ops:
  9.0 9.6 %all-to-all-start = ((f32[32,16,512]{2,1,0:T(8,128)}), f32[32,16,512]{2,1,0:T(8,128)S(1)}, u32[]{:S(2)}, u32[]{:S(2)}) async-start(f32[32,16,512]{2,1,0:T(8,128)} %bitcast.4), calls=%async_computation | async-start | bytes 2097152 | tf_op jit(solution)/shard_map/all_to_all | solution.py:16
  18.6 15.2 %all-to-all-done = f32[32,16,512]{2,1,0:T(8,128)S(1)} async-done(((f32[32,16,512]{2,1,0:T(8,128)}), f32[32,16,512]{2,1,0:T(8,128)S(1)}, u32[]{:S(2)}, u32[]{:S(2)}) %all-to-all-start) | async-done | bytes 1048608 | tf_op jit(solution)/shard_map/all_to_all | solution.py:16
  34.4 13.3 %all-to-all-start.1 = ((f32[16,1,512]{2,1,0:T(1,128)}), f32[16,1,512]{2,1,0:T(1,128)S(1)}, u32[]{:S(2)}, u32[]{:S(2)}) async-start(f32[16,1,512]{2,1,0:T(1,128)} %copy.41), calls=%async_computation.1 | async-start | bytes 65536 | tf_op jit(solution)/shard_map/all_to_all | solution.py:16
  47.9 12.5 %all-to-all-done.1 = f32[16,1,512]{2,1,0:T(1,128)S(1)} async-done(((f32[16,1,512]{2,1,0:T(1,128)}), f32[16,1,512]{2,1,0:T(1,128)S(1)}, u32[]{:S(2)}, u32[]{:S(2)}) %all-to-all-start.1) | async-done | bytes 32800 | tf_op jit(solution)/shard_map/all_to_all | solution.py:16
  61.0 3.5 %all-to-all-start.2 = ((f32[16,16,128]{2,1,0:T(8,128)}), f32[16,16,128]{2,1,0:T(8,128)S(1)}, u32[]{:S(2)}, u32[]{:S(2)}) async-start(f32[16,16,128]{2,1,0:T(8,128)} %broadcast_in_dim.17), calls=%async_computation.2 | async-start | bytes 262144 | tf_op jit(solution)/shard_map/all_to_all | solution.py:16
  64.6 2.0 maximum_select_fusion
  66.6 1.3 copy-done.2
  68.8 2.1 collective-permute-start.1
  71.0 8.3 %collective-permute-start.10 = (f32[32,1024]{1,0:T(8,128)S(1)}, f32[32,1024]{1,0:T(8,128)S(1)}, u32[]{:S(2)}, u32[]{:S(2)}) collective-permute-start(f32[32,1024]{1,0:T(8,128)S(1)} %get-tuple-element.25), channel_id=1, source_target_pairs={{0,352},{32,384},{1,353},{33,385},{2,354},{34,386},{3,355},{35,387... | collective-permute-start | bytes 393224 | tf_op jit(solution)/shard_map/ppermute | solution.py:37
  84.5 6.7 %collective-permute-done.10 = f32[32,1024]{1,0:T(8,128)S(1)} collective-permute-done((f32[32,1024]{1,0:T(8,128)S(1)}, f32[32,1024]{1,0:T(8,128)S(1)}, u32[]{:S(2)}, u32[]{:S(2)}) %collective-permute-start.10) | collective-permute-done | bytes 131104 | tf_op jit(solution)/shard_map/ppermute | solution.py:37
  92.5 1.9 collective-permute-start.2
  94.4 2.8 %collective-permute-done.12 = f32[32,1024]{1,0:T(8,128)S(1)} collective-permute-done((f32[32,1024]{1,0:T(8,128)S(1)}, f32[32,1024]{1,0:T(8,128)S(1)}, u32[]{:S(2)}, u32[]{:S(2)}) %collective-permute-start.12) | collective-permute-done | bytes 131104 | tf_op jit(solution)/shard_map/ppermute | solution.py:37
  100.0 4.6 %collective-permute-done.14 = f32[32,1024]{1,0:T(8,128)S(1)} collective-permute-done((f32[32,1024]{1,0:T(8,128)}, f32[32,1024]{1,0:T(8,128)S(1)}, u32[]{:S(2)}, u32[]{:S(2)}) %collective-permute-start.14) | collective-permute-done | bytes 131104 | tf_op jit(solution)/shard_map/ppermute | solution.py:37
  107.2 1.5 collective-permute-done.2
  113.8 5.1 %all-to-all-start.3 = ((f32[4,96,512]{2,1,0:T(8,128)}), f32[4,96,512]{2,1,0:T(8,128)S(1)}, u32[]{:S(2)}, u32[]{:S(2)}) async-start(f32[4,96,512]{2,1,0:T(8,128)} %broadcast_in_dim.18), calls=%async_computation.3 | async-start | bytes 1572864 | tf_op jit(solution)/shard_map/all_to_all | solution.py:16
  121.1 5.2 %all-to-all-done.3 = f32[4,96,512]{2,1,0:T(8,128)S(1)} async-done(((f32[4,96,512]{2,1,0:T(8,128)}), f32[4,96,512]{2,1,0:T(8,128)S(1)}, u32[]{:S(2)}, u32[]{:S(2)}) %all-to-all-start.3) | async-done | bytes 786464 | tf_op jit(solution)/shard_map/all_to_all | solution.py:16
  126.3 2.2 broadcast_in_dim.19
  128.5 4.8 %all-to-all-start.4 = ((f32[4,4,96,512]{3,2,1,0:T(8,128)}), f32[4,4,96,512]{3,2,1,0:T(8,128)}, u32[]{:S(2)}, u32[]{:S(2)}) async-start(f32[4,4,96,512]{3,2,1,0:T(8,128)} %broadcast_in_dim.19), calls=%async_computation.4 | async-start | bytes 6291456 | tf_op jit(solution)/shard_map/all_to_all | solution.py:16
  134.1 21.4 %all-to-all-done.4 = f32[4,4,96,512]{3,2,1,0:T(8,128)} async-done(((f32[4,4,96,512]{3,2,1,0:T(8,128)}), f32[4,4,96,512]{3,2,1,0:T(8,128)}, u32[]{:S(2)}, u32[]{:S(2)}) %all-to-all-start.4) | async-done | bytes 3145760 | tf_op jit(solution)/shard_map/all_to_all | solution.py:16
  155.5 2.1 collective-permute-start
  164.0 2.5 %copy.52 = f32[512,512]{0,1:T(8,128)} copy(f32[512,512]{1,0:T(8,128)} %get-tuple-element.14) | data formatting | bytes 2097152
  166.5 1.3 copy.53
  169.0 3.6 %broadcast_select_fusion.1 = (f32[16,96,512]{2,1,0:T(8,128)S(1)}, f32[16,96,512]{2,1,0:T(8,128)S(1)}) fusion(f32[16,96,512]{2,1,0:T(8,128)} %collective-permute-done, pred[]{:T(512)S(6)} %eq.77, f32[4,4,96,512]{3,2,1,0:T(8,128)} %all-to-all-done.4), kind=kLoop, calls=%fused_computation.10 | loop fusion | flops 1572864 | bytes 12582913 | tf_op jit(solution)/shard_map/jit(_where)/select_n | solution.py:66
  174.2 1.9 fusion
  178.2 2.0 fusion.10
  180.2 29.8 %all-gather.2.cloned.1.call-done = f32[1024,1024]{1,0:T(8,128)} async-done(((f32[64,1024]{1,0:T(8,128)}), f32[1024,1024]{1,0:T(8,128)}) %all-gather.2.cloned.1.call-update) | async-done | bytes 4194320 | tf_op jit(solution)/shard_map/all_gather | solution.py:81
  210.1 2.7 %fusion.35 = (f32[16,1,32,1024]{3,2,1,0:T(8,128)S(1)}, f32[16,1,32,1024]{3,2,1,0:T(8,128)S(1)}) fusion(f32[16,2,32,1024]{3,2,1,0:T(8,128)} %bitcast.71), kind=kLoop, calls=%fused_computation.75 | loop fusion | bytes 8388608 | tf_op jit(solution)/shard_map/slice | solution.py:83
  212.9 2.3 convolution_subtract_fusion.1
  215.2 1.7 convolution_subtract_fusion
  216.9 2.4 %convolution_subtract_fusion.3 = f32[512,512]{0,1:T(8,128)S(1)} fusion(f32[512,512]{0,1:T(8,128)S(1)} %copy-done.3, f32[512,1024]{1,0:T(8,128)S(1)} %bitcast.69, f32[512,512]{0,1:T(8,128)S(1)} %copy-done.1, f32[1024,512]{0,1:T(8,128)S(1)} %fusion, f32[]{:T(128)} %bitcast.39, f32[]{:T(128)} %bitcast.37, f32[]{:T(128)S(6)} %convert_element_type.24), kind=kOutput, calls=%fused_computation.16 | convolution fusion | flops 806617088 | bytes 5242892 | tf_op jit(solution)/shard_map/dot_general | solution.py:12
  219.3 1.9 fusion.5
  221.3 1.8 copy.50
  (86 shorter events, 33.4 us)
Async XLA Ops:
  7.9 10.7 %copy-start.5 = (f32[2,32,512]{2,1,0:T(8,128)S(1)}, f32[2,32,512]{2,1,0:T(8,128)}, u32[]{:S(2)}) copy-start(f32[2,32,512]{2,1,0:T(8,128)} %param.7) | copy-start | bytes 393220
  9.0 24.8 %all-to-all-start = ((f32[32,16,512]{2,1,0:T(8,128)}), f32[32,16,512]{2,1,0:T(8,128)S(1)}, u32[]{:S(2)}, u32[]{:S(2)}) async-start(f32[32,16,512]{2,1,0:T(8,128)} %bitcast.4), calls=%async_computation | async-start | bytes 2097152 | tf_op jit(solution)/shard_map/all_to_all | solution.py:16
  34.4 25.9 %all-to-all-start.1 = ((f32[16,1,512]{2,1,0:T(1,128)}), f32[16,1,512]{2,1,0:T(1,128)S(1)}, u32[]{:S(2)}, u32[]{:S(2)}) async-start(f32[16,1,512]{2,1,0:T(1,128)} %copy.41), calls=%async_computation.1 | async-start | bytes 65536 | tf_op jit(solution)/shard_map/all_to_all | solution.py:16
  47.8 16.7 %slice-start = ((f32[512,1024]{1,0:T(8,128)}), f32[480,1024]{1,0:T(8,128)S(1)}, s32[]{:S(2)}) async-start(f32[512,1024]{1,0:T(8,128)} %param.6), calls=%async_computation.6 | async-start | bytes 3932160 | tf_op jit(solution)/shard_map/jit(_roll_static)/slice | solution.py:33
  47.8 16.7 %slice-start.1 = ((f32[512,1024]{1,0:T(8,128)}), f32[32,1024]{1,0:T(8,128)S(1)}, s32[]{:S(2)}) async-start(f32[512,1024]{1,0:T(8,128)} %param.6), calls=%async_computation.7 | async-start | bytes 262144 | tf_op jit(solution)/shard_map/jit(_roll_static)/slice | solution.py:33
  61.0 38.9 %all-to-all-start.2 = ((f32[16,16,128]{2,1,0:T(8,128)}), f32[16,16,128]{2,1,0:T(8,128)S(1)}, u32[]{:S(2)}, u32[]{:S(2)}) async-start(f32[16,16,128]{2,1,0:T(8,128)} %broadcast_in_dim.17), calls=%async_computation.2 | async-start | bytes 262144 | tf_op jit(solution)/shard_map/all_to_all | solution.py:16
  66.5 1.3 copy-start.2
  68.8 14.4 %collective-permute-start.1 = (f32[32,1024]{1,0:T(8,128)S(1)}, f32[32,1024]{1,0:T(8,128)S(1)}, u32[]{:S(2)}, u32[]{:S(2)}) collective-permute-start(f32[32,1024]{1,0:T(8,128)S(1)} %get-tuple-element.34), channel_id=1, source_target_pairs={{0,32},{32,64},{1,33},{33,65},{2,34},{34,66},{3,35},{35,67},{4,36}... | collective-permute-start | bytes 393224 | tf_op jit(solution)/shard_map/ppermute | solution.py:37
  71.0 20.3 %collective-permute-start.10 = (f32[32,1024]{1,0:T(8,128)S(1)}, f32[32,1024]{1,0:T(8,128)S(1)}, u32[]{:S(2)}, u32[]{:S(2)}) collective-permute-start(f32[32,1024]{1,0:T(8,128)S(1)} %get-tuple-element.25), channel_id=1, source_target_pairs={{0,352},{32,384},{1,353},{33,385},{2,354},{34,386},{3,355},{35,387... | collective-permute-start | bytes 393224 | tf_op jit(solution)/shard_map/ppermute | solution.py:37
  79.3 13.2 %collective-permute-start.11 = (f32[32,1024]{1,0:T(8,128)S(1)}, f32[32,1024]{1,0:T(8,128)S(1)}, u32[]{:S(2)}, u32[]{:S(2)}) collective-permute-start(f32[32,1024]{1,0:T(8,128)S(1)} %get-tuple-element.24), channel_id=1, source_target_pairs={{0,192},{32,224},{1,193},{33,225},{2,194},{34,226},{3,195},{35,227... | collective-permute-start | bytes 393224 | tf_op jit(solution)/shard_map/ppermute | solution.py:37
  80.6 16.7 %collective-permute-start.12 = (f32[32,1024]{1,0:T(8,128)S(1)}, f32[32,1024]{1,0:T(8,128)S(1)}, u32[]{:S(2)}, u32[]{:S(2)}) collective-permute-start(f32[32,1024]{1,0:T(8,128)S(1)} %get-tuple-element.23), channel_id=1, source_target_pairs={{0,320},{32,352},{1,321},{33,353},{2,322},{34,354},{3,323},{35,355... | collective-permute-start | bytes 393224 | tf_op jit(solution)/shard_map/ppermute | solution.py:37
  81.9 16.7 %collective-permute-start.13 = (f32[32,1024]{1,0:T(8,128)S(1)}, f32[32,1024]{1,0:T(8,128)S(1)}, u32[]{:S(2)}, u32[]{:S(2)}) collective-permute-start(f32[32,1024]{1,0:T(8,128)S(1)} %get-tuple-element.22), channel_id=1, source_target_pairs={{0,224},{32,256},{1,225},{33,257},{2,226},{34,258},{3,227},{35,259... | collective-permute-start | bytes 393224 | tf_op jit(solution)/shard_map/ppermute | solution.py:37
  83.2 21.3 %collective-permute-start.14 = (f32[32,1024]{1,0:T(8,128)}, f32[32,1024]{1,0:T(8,128)S(1)}, u32[]{:S(2)}, u32[]{:S(2)}) collective-permute-start(f32[32,1024]{1,0:T(8,128)} %get-tuple-element.21), channel_id=1, source_target_pairs={{0,288},{32,320},{1,289},{33,321},{2,290},{34,322},{3,291},{35,323... | collective-permute-start | bytes 393224 | tf_op jit(solution)/shard_map/ppermute | solution.py:37
  91.2 14.6 %collective-permute-start.15 = (f32[32,1024]{1,0:T(8,128)S(1)}, f32[32,1024]{1,0:T(8,128)S(1)}, u32[]{:S(2)}, u32[]{:S(2)}) collective-permute-start(f32[32,1024]{1,0:T(8,128)S(1)} %get-tuple-element.20), channel_id=1, source_target_pairs={{0,256},{32,288},{1,257},{33,289},{2,258},{34,290},{3,259},{35,291... | collective-permute-start | bytes 393224 | tf_op jit(solution)/shard_map/ppermute | solution.py:37
  92.5 16.2 %collective-permute-start.2 = (f32[32,1024]{1,0:T(8,128)S(1)}, f32[32,1024]{1,0:T(8,128)S(1)}, u32[]{:S(2)}, u32[]{:S(2)}) collective-permute-start(f32[32,1024]{1,0:T(8,128)S(1)} %get-tuple-element.33), channel_id=1, source_target_pairs={{0,480},{32,0},{1,481},{33,1},{2,482},{34,2},{3,483},{35,3},{4,484... | collective-permute-start | bytes 393224 | tf_op jit(solution)/shard_map/ppermute | solution.py:37
  97.3 12.7 %collective-permute-start.3 = (f32[32,1024]{1,0:T(8,128)S(1)}, f32[32,1024]{1,0:T(8,128)S(1)}, u32[]{:S(2)}, u32[]{:S(2)}) collective-permute-start(f32[32,1024]{1,0:T(8,128)S(1)} %get-tuple-element.32), channel_id=1, source_target_pairs={{0,64},{32,96},{1,65},{33,97},{2,66},{34,98},{3,67},{35,99},{4,68}... | collective-permute-start | bytes 393224 | tf_op jit(solution)/shard_map/ppermute | solution.py:37
  98.6 12.9 %collective-permute-start.4 = (f32[32,1024]{1,0:T(8,128)S(1)}, f32[32,1024]{1,0:T(8,128)S(1)}, u32[]{:S(2)}, u32[]{:S(2)}) collective-permute-start(f32[32,1024]{1,0:T(8,128)S(1)} %get-tuple-element.31), channel_id=1, source_target_pairs={{0,448},{32,480},{1,449},{33,481},{2,450},{34,482},{3,451},{35,483... | collective-permute-start | bytes 393224 | tf_op jit(solution)/shard_map/ppermute | solution.py:37
  104.6 14.3 %collective-permute-start.5 = (f32[32,1024]{1,0:T(8,128)}, f32[32,1024]{1,0:T(8,128)S(1)}, u32[]{:S(2)}, u32[]{:S(2)}) collective-permute-start(f32[32,1024]{1,0:T(8,128)} %get-tuple-element.30), channel_id=1, source_target_pairs={{0,96},{32,128},{1,97},{33,129},{2,98},{34,130},{3,99},{35,131},{4... | collective-permute-start | bytes 393224 | tf_op jit(solution)/shard_map/ppermute | solution.py:37
  105.9 13.0 %collective-permute-start.6 = (f32[32,1024]{1,0:T(8,128)}, f32[32,1024]{1,0:T(8,128)S(1)}, u32[]{:S(2)}, u32[]{:S(2)}) collective-permute-start(f32[32,1024]{1,0:T(8,128)} %get-tuple-element.29), channel_id=1, source_target_pairs={{0,416},{32,448},{1,417},{33,449},{2,418},{34,450},{3,419},{35,451... | collective-permute-start | bytes 393224 | tf_op jit(solution)/shard_map/ppermute | solution.py:37
  108.7 10.2 %collective-permute-start.7 = (f32[32,1024]{1,0:T(8,128)}, f32[32,1024]{1,0:T(8,128)S(1)}, u32[]{:S(2)}, u32[]{:S(2)}) collective-permute-start(f32[32,1024]{1,0:T(8,128)} %get-tuple-element.28), channel_id=1, source_target_pairs={{0,128},{32,160},{1,129},{33,161},{2,130},{34,162},{3,131},{35,163... | collective-permute-start | bytes 393224 | tf_op jit(solution)/shard_map/ppermute | solution.py:37
  110.0 8.9 %collective-permute-start.8 = (f32[32,1024]{1,0:T(8,128)S(1)}, f32[32,1024]{1,0:T(8,128)S(1)}, u32[]{:S(2)}, u32[]{:S(2)}) collective-permute-start(f32[32,1024]{1,0:T(8,128)S(1)} %get-tuple-element.27), channel_id=1, source_target_pairs={{0,384},{32,416},{1,385},{33,417},{2,386},{34,418},{3,387},{35,419... | collective-permute-start | bytes 393224 | tf_op jit(solution)/shard_map/ppermute | solution.py:37
  111.5 7.5 %collective-permute-start.9 = (f32[32,1024]{1,0:T(8,128)S(1)}, f32[32,1024]{1,0:T(8,128)S(1)}, u32[]{:S(2)}, u32[]{:S(2)}) collective-permute-start(f32[32,1024]{1,0:T(8,128)S(1)} %get-tuple-element.26), channel_id=1, source_target_pairs={{0,160},{32,192},{1,161},{33,193},{2,162},{34,194},{3,163},{35,195... | collective-permute-start | bytes 393224 | tf_op jit(solution)/shard_map/ppermute | solution.py:37
  113.8 12.5 %all-to-all-start.3 = ((f32[4,96,512]{2,1,0:T(8,128)}), f32[4,96,512]{2,1,0:T(8,128)S(1)}, u32[]{:S(2)}, u32[]{:S(2)}) async-start(f32[4,96,512]{2,1,0:T(8,128)} %broadcast_in_dim.18), calls=%async_computation.3 | async-start | bytes 1572864 | tf_op jit(solution)/shard_map/all_to_all | solution.py:16
  128.5 29.1 %copy-start.7 = (s32[2,64]{1,0:T(2,128)S(1)}, s32[2,64]{1,0:T(2,128)}, u32[]{:S(2)}) copy-start(s32[2,64]{1,0:T(2,128)} %param.9) | copy-start | bytes 1540
  128.5 30.4 %copy-start.6 = (s32[2,16]{1,0:T(2,128)S(1)}, s32[2,16]{1,0:T(2,128)}, u32[]{:S(2)}) copy-start(s32[2,16]{1,0:T(2,128)} %param.8) | copy-start | bytes 388
  128.5 34.3 %copy-start = (f32[512,1024]{1,0:T(8,128)S(1)}, f32[512,1024]{1,0:T(8,128)}, u32[]{:S(2)}) copy-start(f32[512,1024]{1,0:T(8,128)} %param.6) | copy-start | bytes 6291460
  128.5 27.0 %all-to-all-start.4 = ((f32[4,4,96,512]{3,2,1,0:T(8,128)}), f32[4,4,96,512]{3,2,1,0:T(8,128)}, u32[]{:S(2)}, u32[]{:S(2)}) async-start(f32[4,4,96,512]{3,2,1,0:T(8,128)} %broadcast_in_dim.19), calls=%async_computation.4 | async-start | bytes 6291456 | tf_op jit(solution)/shard_map/all_to_all | solution.py:16
  133.3 76.8 %all-gather.2.cloned.1.call-start = ((), (), s32[]{:S(2)}) async-start(), calls=%async_computation.5 | async-start | bytes 4456448 | tf_op jit(solution)/shard_map/all_gather | solution.py:81
  155.5 13.5 %collective-permute-start = (f32[16,96,512]{2,1,0:T(8,128)}, f32[16,96,512]{2,1,0:T(8,128)}, u32[]{:S(2)}, u32[]{:S(2)}) collective-permute-start(f32[16,96,512]{2,1,0:T(8,128)} %bitcast.22), channel_id=1, source_target_pairs={{0,1},{1,0},{2,3},{3,2},{4,5},{5,4},{6,7},{7,6},{8,9},{9,8},{10,11... | collective-permute-start | bytes 9437192 | tf_op jit(solution)/shard_map/ppermute | solution.py:65
  210.0 2.7 %copy-start.1 = (f32[512,512]{0,1:T(8,128)S(1)}, f32[512,512]{0,1:T(8,128)}, u32[]{:S(2)}) copy-start(f32[512,512]{0,1:T(8,128)} %fusion.10) | copy-start | bytes 3145732
  210.1 2.8 %copy-start.4 = (f32[512,512]{0,1:T(8,128)S(1)}, f32[512,512]{0,1:T(8,128)}, u32[]{:S(2)}) copy-start(f32[512,512]{0,1:T(8,128)} %copy.53) | copy-start | bytes 3145732
  215.2 1.7 copy-start.3
Sparse Core Ops, SparseCore 0:
  136.2 73.8 all-gather.1

commit v2 on v1

--- a/solution.py
+++ b/solution.py
@@ -1,6 +1,10 @@
+import functools
+
 import jax
 import jax.numpy as jnp
 from jax import lax
+from jax.experimental import pallas as pl
+from jax.experimental.pallas import tpu as pltpu
 from jax.sharding import PartitionSpec as P
 
 
@@ -24,7 +28,7 @@
 
 def send_order(count):
     half = [d for i in range(1, count // 2) for d in (i, count - i)]
-    return [count // 2, *reversed(half)]
+    return [*half, count // 2]
 
 
 def scatter_rows(matrix):
@@ -38,6 +42,26 @@
         first = jnp.where(here == d, came, first)
         second = jnp.where(here == (1 + d) % count, came, second)
     return jnp.concatenate([first, second], axis=0)
+
+
+def tree_copies(own):
+    count, here = lax.axis_size(ROWS), lax.axis_index(ROWS)
+    held = own
+    for c in range(4, count, 4):
+        came = lax.ppermute(own, ROWS, [(0, c), (1, c + 1)])
+        held = jnp.where((here == c) | (here == c + 1), came, held)
+    leaves = [held]
+    for step in (1, 2, -1):
+        pairs = [((c + k) % count, (c + k + step) % count) for c in range(0, count, 4) for k in (0, 1)]
+        leaves.append(lax.ppermute(held, ROWS, pairs))
+
+    def of(place):
+        found = leaves[0]
+        for i in (1, 2, 3):
+            found = jnp.where(place % 4 == i, leaves[i], found)
+        return found
+
+    return of(here), of(here + 3)
 
 
 def plane(count):
@@ -67,6 +91,54 @@
     return jnp.concatenate([low, high], axis=0)
 
 
+def halves(x):
+    high = x.astype(jnp.bfloat16)
+    return high, (x - high.astype(jnp.float32)).astype(jnp.bfloat16)
+
+
+def update_kernel(steps, length, keeps, matrix, raw, left, stored, out, high, low):
+    step = pl.program_id(0)
+
+    @pl.when(step % steps == 0)
+    def _():
+        high[...], low[...] = halves(left[0])
+
+    rows = raw.shape[0]
+    starts = [*range(0, rows, 2 * length), *range(length, rows, 2 * length)]
+    split = [jnp.concatenate([x[i : i + length] for i in starts]) for x in halves(raw[...])]
+    dot = functools.partial(jnp.dot, preferred_element_type=jnp.float32)
+    product = dot(high[...], split[0]) + (dot(high[...], split[1]) + dot(low[...], split[0]))
+    new = matrix[...] - product
+    out[...] = jnp.where((keeps[0] == 1) & (step < steps), stored[...], new)
+
+
+def update(keeps, matrix, raw, left, stored, length):
+    rows, width = stored.shape
+    cols = matrix.shape[1]
+    wide = min(256, width)
+    steps = width // wide
+    return pl.pallas_call(
+        functools.partial(update_kernel, steps, length),
+        grid_spec=pltpu.PrefetchScalarGridSpec(
+            num_scalar_prefetch=1,
+            grid=(cols // wide,),
+            in_specs=[
+                pl.BlockSpec((rows, wide), lambda t, _: (0, t)),
+                pl.BlockSpec((2 * rows, wide), lambda t, _: (0, t)),
+                pl.BlockSpec((1, rows, 2 * rows), lambda t, _: (t // steps, 0, 0)),
+                pl.BlockSpec((rows, wide), lambda t, _: (0, jnp.minimum(t, steps - 1))),
+            ],
+            out_specs=pl.BlockSpec((rows, wide), lambda t, _: (0, t)),
+            scratch_shapes=[pltpu.VMEM((rows, 2 * rows), jnp.bfloat16)] * 2,
+        ),
+        out_shape=jax.ShapeDtypeStruct(matrix.shape, jnp.float32),
+        cost_estimate=pl.CostEstimate(
+            flops=12 * rows * rows * cols, bytes_accessed=32 * rows * cols, transcendentals=0
+        ),
+        name="update",
+    )(keeps, matrix, raw, left, stored)
+
+
 def per_device(matrix, pivot_inverse, row_live, col_live):
     width = pivot_inverse.shape[2]
     n_rows, n_cols = lax.axis_size(ROWS), lax.axis_size(COLS)
@@ -78,25 +150,19 @@
     spread = exchange(holders(matrix[:, :width].reshape(n_cols, lines, width)), COLS)
     mine = spread[:2]
 
-    raw = lax.all_gather(scatter_rows(matrix), ROWS, axis=0, tiled=True)
-    raw = raw.reshape(n_rows, 2, -1, matrix.shape[1])
-    raw0, raw1 = raw[:, 0].reshape(matrix.shape), raw[:, 1].reshape(matrix.shape)
-
-    sent = jnp.where(g == 0, mine[1], mine[0]).reshape(n_rows, lines // n_rows, width)
-    got = exchange(sent, ROWS)[:2]
+    pieces = scatter_rows(matrix)
+    raw = lax.all_gather(pieces, ROWS, axis=0, tiled=True)
+
+    cross = tree_copies(jnp.where(g == 0, mine[1], mine[0]))
     tiles = pivot_inverse.reshape(2, row_groups, TILE, col_groups, lane)
     tiles = tiles.transpose(0, 1, 3, 2, 4).reshape(n_cols, TILE, lane)
     tile = lax.dynamic_index_in_dim(holders(tiles), p, keepdims=False)
-    small = jnp.concatenate([got.reshape(-1, lane), tile], axis=0)
-    split = got.size // lane
-    small = exchange(copies(small, n_rows), ROWS)
-    cross = small[:, :split].reshape(n_rows, 2, lines // n_rows, width)
-    cross = cross.transpose(1, 0, 2, 3).reshape(2 * lines, width)
+    pivots = exchange(copies(tile, n_rows), ROWS)
     wide = width // lane
-    pivots = small[:, split:].reshape(n_rows // wide, wide, TILE, lane)
+    pivots = pivots.reshape(n_rows // wide, wide, TILE, lane)
     pivots = pivots.transpose(0, 2, 1, 3).reshape(-1, width)
 
-    piece = jnp.concatenate([mine.reshape(2 * lines, width), cross, pivots], axis=0)
+    piece = jnp.concatenate([*mine, *cross, pivots], axis=0)
     shared = gather_plane(piece)
     a_g0, a_g1, a_01, a_10 = (
         shared[:, i * lines : (i + 1) * lines].reshape(width, width) for i in range(4)
@@ -123,17 +189,15 @@
     lower1 = matmul(a_g1, inverse[1]) * lower(1, g)
     mixed = matmul(lower1, pivot_lower)
 
-    out = []
-    for j in range(matrix.shape[1] // width):
-        span = slice(j * width, (j + 1) * width)
-        left0 = (lower0 - mixed * up1[j]) * up0[j]
-        block = matrix[:, span] - matmul(left0, raw0[:, span])
-        block = block - matmul(lower1 * up1[j], raw1[:, span])
-        if j == 0:
-            block = jnp.where((p == 0) & (g > 0), lower0, block)
-            block = jnp.where((p == 1) & (g > 1), lower1, block)
-        out.append(block)
-    return jnp.concatenate(out, axis=1)
+    left = jnp.stack(
+        [
+            jnp.concatenate([(lower0 - mixed * up1[j]) * up0[j], lower1 * up1[j]], axis=1)
+            for j in range(matrix.shape[1] // width)
+        ]
+    )
+    stored = jnp.where(p == 0, lower0, lower1)
+    keeps = jnp.where(p == 0, g > 0, (p == 1) & (g > 1)).astype(jnp.int32).reshape(1)
+    return update(keeps, matrix, raw, left, stored, length=width // n_rows)
 
 
 def solution(mesh):

time: 231 us -> 226 us (0.978)
  waiting for transfers between devices: 99.8 us -> 70.7 us
  starting transfers between devices: 66.3 us -> 86.3 us
  Pallas kernels: 0 us -> 9.05 us
  local copies, waits for them, and re-layouts: 23 us -> 18.6 us
  matrix products: 14.2 us -> 9.98 us
  other arithmetic: 9.93 us -> 12.8 us
    ppermute x0 -> x6, starting transfers between devices: none -> 25.2 us  [the longest x3 15.8 us: tree_copies(): came = lax.ppermute(own, ROWS, [(0, c), (1, c + 1)])]
    all_to_all x5 -> x4, waiting for transfers between devices: 54.2 us -> 35.3 us  [exchange(): lax.all_to_all(pieces, axis, split_axis=0, concat_axis=0, tiled=True, axi...]
    all_to_all x5 -> x4, starting transfers between devices: 36.3 us -> 22.5 us  [exchange(): lax.all_to_all(pieces, axis, split_axis=0, concat_axis=0, tiled=True, axi...]
    ppermute x15, waiting for transfers between devices: 15.8 us -> 2.25 us  [scatter_rows(): came = lax.ppermute(turned[d * length:(d + 1) * length], ROWS, pairs)]
    pallas_call x0 -> x1, Pallas kernels: none -> 9.05 us  [update(): pl.pallas_call(functools.partial(update_kernel, steps, length), grid_spec...]
    ppermute x15, starting transfers between devices: 27.9 us -> 36.5 us  [scatter_rows(): came = lax.ppermute(turned[d * length:(d + 1) * length], ROWS, pairs)]
    dot_general x8 -> x4, matrix products: 14.2 us -> 9.98 us  [matmul(): return jnp.dot(a, b, precision=lax.Precision.HIGH)]
    slice x7 -> x3, local copies, waits for them, and re-layouts: 5.02 us -> 2.31 us  [the longest x1 1.11 us: per_device(): lower0 = both[:width] * lower(0, g)]
  transfers between devices with their start and end apart: 22 -> 27, of which waited for: 10 -> 6; matrix products, arithmetic and copies ran while one was open for 12% -> 16% of each run, Pallas kernels for 0% -> 0%
where the time goes in v2:
time: 226 us; the launch traced here: 224 us
  starting transfers between devices  86.3 us (38%)
  waiting for transfers between devices  70.7 us (31%)
  local copies, waits for them, and re-layouts  18.6 us (8%)
  between operations  16.9 us (7%)
  other arithmetic  12.8 us (6%)
  matrix products  9.98 us (4%)
  Pallas kernels  9.05 us (4%)
    ppermute x15, starting transfers between devices, scatter_rows(): came = lax.ppermute(turned[d * length:(d + 1) * length], ROWS, pairs)  36.5 us
    all_to_all x4, waiting for transfers between devices, exchange(): lax.all_to_all(pieces, axis, split_axis=0, concat_axis=0, tiled=True, axi...  35.3 us
    all_gather x1, waiting for transfers between devices, per_device(): raw = lax.all_gather(pieces, ROWS, axis=0, tiled=True)  31.6 us
    all_to_all x4, starting transfers between devices, exchange(): lax.all_to_all(pieces, axis, split_axis=0, concat_axis=0, tiled=True, axi...  22.5 us
    ppermute x3, starting transfers between devices, tree_copies(): came = lax.ppermute(own, ROWS, [(0, c), (1, c + 1)])  15.8 us
    dot_general x4, matrix products, matmul(): return jnp.dot(a, b, precision=lax.Precision.HIGH)  9.98 us
    ppermute x3, starting transfers between devices, tree_copies(): leaves.append(lax.ppermute(held, ROWS, pairs))  9.38 us
    pallas_call x1, Pallas kernels, update(): pl.pallas_call(functools.partial(update_kernel, steps, length), grid_spec...  9.05 us
  transfers between devices with their start and end apart: 27, of which 6 were waited for; matrix products, arithmetic and copies ran while one was open for 16% of the time, Pallas kernels for 0%

profile of v2, /device:TPU:6, one launch (start us, length us, event | category | flops | bytes accessed | tf_op | source)
XLA Modules:
  0.0 224.3 jit_solution(917111219253116173)
XLA Ops:
  9.0 9.6 %all-to-all-start = ((f32[32,16,512]{2,1,0:T(8,128)}), f32[32,16,512]{2,1,0:T(8,128)S(1)}, u32[]{:S(2)}, u32[]{:S(2)}) async-start(f32[32,16,512]{2,1,0:T(8,128)} %bitcast.5), calls=%async_computation | async-start | bytes 2097152 | tf_op jit(solution)/shard_map/all_to_all | solution.py:20
  18.6 15.1 %all-to-all-done = f32[32,16,512]{2,1,0:T(8,128)S(1)} async-done(((f32[32,16,512]{2,1,0:T(8,128)}), f32[32,16,512]{2,1,0:T(8,128)S(1)}, u32[]{:S(2)}, u32[]{:S(2)}) %all-to-all-start) | async-done | bytes 1048608 | tf_op jit(solution)/shard_map/all_to_all | solution.py:20
  33.8 10.9 %collective-permute-start.15 = (f32[16,512]{1,0:T(8,128)S(1)}, f32[16,512]{1,0:T(8,128)S(1)}, u32[]{:S(2)}, u32[]{:S(2)}) collective-permute-start(f32[16,512]{1,0:T(8,128)S(1)} %get-tuple-element.36), channel_id=1, source_target_pairs={{0,384},{32,416},{1,385},{33,417},{2,386},{34,418},{3,387},{35,419... | collective-permute-start | bytes 98312 | tf_op jit(solution)/shard_map/ppermute | solution.py:51
  44.7 3.7 %collective-permute-start.16 = (f32[16,512]{1,0:T(8,128)S(1)}, f32[16,512]{1,0:T(8,128)S(1)}, u32[]{:S(2)}, u32[]{:S(2)}) collective-permute-start(f32[16,512]{1,0:T(8,128)S(1)} %get-tuple-element.36), channel_id=1, source_target_pairs={{0,256},{32,288},{1,257},{33,289},{2,258},{34,290},{3,259},{35,291... | collective-permute-start | bytes 98312 | tf_op jit(solution)/shard_map/ppermute | solution.py:51
  50.3 3.5 %all-to-all-start.1 = ((f32[16,8,128]{2,1,0:T(8,128)}), f32[16,8,128]{2,1,0:T(8,128)S(1)}, u32[]{:S(2)}, u32[]{:S(2)}) async-start(f32[16,8,128]{2,1,0:T(8,128)} %broadcast_in_dim.17), calls=%async_computation.1 | async-start | bytes 131072 | tf_op jit(solution)/shard_map/all_to_all | solution.py:20
  53.9 5.1 %collective-permute-start.18 = (f32[16,512]{1,0:T(8,128)S(1)}, f32[16,512]{1,0:T(8,128)S(1)}, u32[]{:S(2)}, u32[]{:S(2)}) collective-permute-start(f32[16,512]{1,0:T(8,128)S(1)} %select_select_fusion.2), channel_id=1, source_target_pairs={{0,480},{32,0},{128,96},{160,128},{256,224},{288,256},{384,352},{4... | collective-permute-start | bytes 98312 | tf_op jit(solution)/shard_map/ppermute | solution.py:56
  60.3 3.0 %collective-permute-start.20 = (f32[16,512]{1,0:T(8,128)S(1)}, f32[16,512]{1,0:T(8,128)S(1)}, u32[]{:S(2)}, u32[]{:S(2)}) collective-permute-start(f32[16,512]{1,0:T(8,128)S(1)} %select_select_fusion.2), channel_id=1, source_target_pairs={{0,32},{32,64},{128,160},{160,192},{256,288},{288,320},{384,416},{... | collective-permute-start | bytes 98312 | tf_op jit(solution)/shard_map/ppermute | solution.py:56
  67.5 5.7 %all-to-all-start.2 = ((f32[4,96,512]{2,1,0:T(8,128)}), f32[4,96,512]{2,1,0:T(8,128)S(1)}, u32[]{:S(2)}, u32[]{:S(2)}) async-start(f32[4,96,512]{2,1,0:T(8,128)} %broadcast_in_dim.18), calls=%async_computation.2 | async-start | bytes 1572864 | tf_op jit(solution)/shard_map/all_to_all | solution.py:20
  73.2 2.0 maximum_select_fusion
  77.4 8.2 %collective-permute-start = (f32[32,1024]{1,0:T(8,128)S(1)}, f32[32,1024]{1,0:T(8,128)S(1)}, u32[]{:S(2)}, u32[]{:S(2)}) collective-permute-start(f32[32,1024]{1,0:T(8,128)S(1)} %get-tuple-element.32), channel_id=1, source_target_pairs={{0,256},{32,288},{1,257},{33,289},{2,258},{34,290},{3,259},{35,291... | collective-permute-start | bytes 393224 | tf_op jit(solution)/shard_map/ppermute | solution.py:41
  85.7 2.1 collective-permute-start.1
  91.7 1.9 collective-permute-start.13
  93.7 2.2 collective-permute-done.1
  95.9 1.7 collective-permute-start.14
  98.9 6.2 %collective-permute-start.3 = (f32[32,1024]{1,0:T(8,128)S(1)}, f32[32,1024]{1,0:T(8,128)S(1)}, u32[]{:S(2)}, u32[]{:S(2)}) collective-permute-start(f32[32,1024]{1,0:T(8,128)S(1)} %get-tuple-element.29), channel_id=1, source_target_pairs={{0,320},{32,352},{1,321},{33,353},{2,322},{34,354},{3,323},{35,355... | collective-permute-start | bytes 393224 | tf_op jit(solution)/shard_map/ppermute | solution.py:41
  106.5 2.0 collective-permute-start.5
  108.5 2.0 collective-permute-start.6
  110.5 1.9 collective-permute-start.7
  112.4 1.9 collective-permute-start.8
  115.0 1.9 collective-permute-start.9
  117.0 2.1 broadcast_in_dim.19
  119.0 3.7 %all-to-all-start.3 = ((f32[4,4,96,512]{3,2,1,0:T(8,128)}), f32[4,4,96,512]{3,2,1,0:T(8,128)S(1)}, u32[]{:S(2)}, u32[]{:S(2)}) async-start(f32[4,4,96,512]{3,2,1,0:T(8,128)} %broadcast_in_dim.19), calls=%async_computation.3 | async-start | bytes 6291456 | tf_op jit(solution)/shard_map/all_to_all | solution.py:20
  126.2 18.6 %all-to-all-done.3 = f32[4,4,96,512]{3,2,1,0:T(8,128)S(1)} async-done(((f32[4,4,96,512]{3,2,1,0:T(8,128)}), f32[4,4,96,512]{3,2,1,0:T(8,128)S(1)}, u32[]{:S(2)}, u32[]{:S(2)}) %all-to-all-start.3) | async-done | bytes 3145760 | tf_op jit(solution)/shard_map/all_to_all | solution.py:20
  144.8 2.1 collective-permute-start.21
  153.4 2.8 %broadcast_select_fusion = (f32[16,96,512]{2,1,0:T(8,128)S(1)}, f32[16,96,512]{2,1,0:T(8,128)S(1)}) fusion(f32[16,96,512]{2,1,0:T(8,128)} %collective-permute-done.21, pred[]{:T(512)S(6)} %eq.125, f32[4,4,96,512]{3,2,1,0:T(8,128)S(1)} %all-to-all-done.3), kind=kLoop, calls=%fused_computation.15 | loop fusion | flops 1572864 | bytes 12582913 | tf_op jit(solution)/shard_map/jit(_where)/select_n | solution.py:90
  157.8 1.8 pad_maximum_fusion.3
  159.6 1.9 fusion.1
  167.0 2.4 %broadcast_multiply_fusion.1 = (f32[512,512]{1,0:T(8,128)S(1)}, f32[512,512]{1,0:T(8,128)S(1)}, f32[512,512]{1,0:T(8,128)S(1)}) fusion(f32[]{:T(128)} %bitcast.35, f32[]{:T(128)} %bitcast.39, f32[]{:T(128)S(6)} %convert_element_type.28, f32[512,512]{1,0:T(8,128)S(1)} %bitcast_subtract_fusion, f32[512,512]{1,0:T(8,128)S(1)} %bitcast.76), kind=kOutput, calls=%fused_computation.33 | convolution fusion | flops 806092800 | bytes 5242892 | tf_op jit(solution)/shard_map/dot_general | solution.py:16
  169.5 4.7 %subtract_multiply_fusion.1 = (f32[512,512]{1,0:T(8,128)S(1)}, f32[512,512]{1,0:T(8,128)S(1)}, f32[512,512]{1,0:T(8,128)}) fusion(f32[512,512]{1,0:T(8,128)S(1)} %copy.35, f32[]{:T(128)} %bitcast.37, f32[]{:T(128)} %bitcast.35, f32[]{:T(128)S(6)} %convert_element_type.25, f32[]{:T(128)} %bitcast.40, f32[]{:T(128)} %bitcast.39, ...), kind=kOutput, calls=%fused_computation.28 | convolution fusion | flops 807665664 | bytes 7340057 | tf_op jit(solution)/shard_map/dot_general | solution.py:16
  174.5 2.3 %pad_maximum_fusion.left = f32[2,512,1024]{2,1,0:T(8,128)} fusion(f32[1,512,1024]{2,1,0:T(8,128)S(1)} %maximum_bitcast_fusion.1, f32[1,512,1024]{2,1,0:T(8,128)S(1)} %maximum_bitcast_fusion), kind=kLoop, calls=%fused_computation.6 | loop fusion | flops 1048576 | bytes 8388608 | tf_op jit(solution)/shard_map/stack | solution.py:192
  176.8 31.6 %all-gather.2.cloned.1.call-done.raw = f32[1024,1024]{1,0:T(8,128)} async-done(((f32[64,1024]{1,0:T(8,128)}), f32[1024,1024]{1,0:T(8,128)}) %all-gather.2.cloned.1.call-update) | async-done | bytes 4194320 | tf_op jit(solution)/shard_map/all_gather | solution.py:154
  208.4 9.0 %update.1 = f32[512,1024]{1,0:T(8,128)} custom-call(s32[1]{0:T(128)} %bitcast.keeps, f32[512,1024]{1,0:T(8,128)} %matrix.1, f32[1024,1024]{1,0:T(8,128)} %all-gather.2.cloned.1.call-done.raw, f32[2,512,1024]{2,1,0:T(8,128)} %pad_maximum_fusion.left, f32[512,512]{1,0:T(8,128)} %get-tuple-element.33.stored), custom_call_target="tpu_custom_call" | custom-call | flops 3221225472 | bytes 16777216 | tf_op jit(solution)/shard_map/update/pallas_call | solution.py:120
  (113 shorter events, 33.7 us)
Async XLA Ops:
  9.0 24.8 %all-to-all-start = ((f32[32,16,512]{2,1,0:T(8,128)}), f32[32,16,512]{2,1,0:T(8,128)S(1)}, u32[]{:S(2)}, u32[]{:S(2)}) async-start(f32[32,16,512]{2,1,0:T(8,128)} %bitcast.5), calls=%async_computation | async-start | bytes 2097152 | tf_op jit(solution)/shard_map/all_to_all | solution.py:20
  33.8 20.1 %collective-permute-start.15 = (f32[16,512]{1,0:T(8,128)S(1)}, f32[16,512]{1,0:T(8,128)S(1)}, u32[]{:S(2)}, u32[]{:S(2)}) collective-permute-start(f32[16,512]{1,0:T(8,128)S(1)} %get-tuple-element.36), channel_id=1, source_target_pairs={{0,384},{32,416},{1,385},{33,417},{2,386},{34,418},{3,387},{35,419... | collective-permute-start | bytes 98312 | tf_op jit(solution)/shard_map/ppermute | solution.py:51
  44.7 9.2 %collective-permute-start.16 = (f32[16,512]{1,0:T(8,128)S(1)}, f32[16,512]{1,0:T(8,128)S(1)}, u32[]{:S(2)}, u32[]{:S(2)}) collective-permute-start(f32[16,512]{1,0:T(8,128)S(1)} %get-tuple-element.36), channel_id=1, source_target_pairs={{0,256},{32,288},{1,257},{33,289},{2,258},{34,290},{3,259},{35,291... | collective-permute-start | bytes 98312 | tf_op jit(solution)/shard_map/ppermute | solution.py:51
  48.3 5.6 %collective-permute-start.17 = (f32[16,512]{1,0:T(8,128)S(1)}, f32[16,512]{1,0:T(8,128)S(1)}, u32[]{:S(2)}, u32[]{:S(2)}) collective-permute-start(f32[16,512]{1,0:T(8,128)S(1)} %get-tuple-element.36), channel_id=1, source_target_pairs={{0,128},{32,160},{1,129},{33,161},{2,130},{34,162},{3,131},{35,163... | collective-permute-start | bytes 98312 | tf_op jit(solution)/shard_map/ppermute | solution.py:51
  50.3 16.2 %all-to-all-start.1 = ((f32[16,8,128]{2,1,0:T(8,128)}), f32[16,8,128]{2,1,0:T(8,128)S(1)}, u32[]{:S(2)}, u32[]{:S(2)}) async-start(f32[16,8,128]{2,1,0:T(8,128)} %broadcast_in_dim.17), calls=%async_computation.1 | async-start | bytes 131072 | tf_op jit(solution)/shard_map/all_to_all | solution.py:20
  53.8 19.4 %slice-start = ((f32[512,1024]{1,0:T(8,128)}), f32[480,1024]{1,0:T(8,128)S(1)}, s32[]{:S(2)}) async-start(f32[512,1024]{1,0:T(8,128)} %matrix.1), calls=%async_computation.5 | async-start | bytes 3932160 | tf_op jit(solution)/shard_map/jit(_roll_static)/slice | solution.py:37
  53.8 19.4 %slice-start.1 = ((f32[512,1024]{1,0:T(8,128)}), f32[32,1024]{1,0:T(8,128)S(1)}, s32[]{:S(2)}) async-start(f32[512,1024]{1,0:T(8,128)} %matrix.1), calls=%async_computation.6 | async-start | bytes 262144 | tf_op jit(solution)/shard_map/jit(_roll_static)/slice | solution.py:37
  53.9 9.4 %collective-permute-start.18 = (f32[16,512]{1,0:T(8,128)S(1)}, f32[16,512]{1,0:T(8,128)S(1)}, u32[]{:S(2)}, u32[]{:S(2)}) collective-permute-start(f32[16,512]{1,0:T(8,128)S(1)} %select_select_fusion.2), channel_id=1, source_target_pairs={{0,480},{32,0},{128,96},{160,128},{256,224},{288,256},{384,352},{4... | collective-permute-start | bytes 98312 | tf_op jit(solution)/shard_map/ppermute | solution.py:56
  59.0 4.3 %collective-permute-start.19 = (f32[16,512]{1,0:T(8,128)S(1)}, f32[16,512]{1,0:T(8,128)S(1)}, u32[]{:S(2)}, u32[]{:S(2)}) collective-permute-start(f32[16,512]{1,0:T(8,128)S(1)} %select_select_fusion.2), channel_id=1, source_target_pairs={{0,64},{32,96},{128,192},{160,224},{256,320},{288,352},{384,448},{... | collective-permute-start | bytes 98312 | tf_op jit(solution)/shard_map/ppermute | solution.py:56
  60.3 4.6 %collective-permute-start.20 = (f32[16,512]{1,0:T(8,128)S(1)}, f32[16,512]{1,0:T(8,128)S(1)}, u32[]{:S(2)}, u32[]{:S(2)}) collective-permute-start(f32[16,512]{1,0:T(8,128)S(1)} %select_select_fusion.2), channel_id=1, source_target_pairs={{0,32},{32,64},{128,160},{160,192},{256,288},{288,320},{384,416},{... | collective-permute-start | bytes 98312 | tf_op jit(solution)/shard_map/ppermute | solution.py:56
  67.5 49.5 %all-to-all-start.2 = ((f32[4,96,512]{2,1,0:T(8,128)}), f32[4,96,512]{2,1,0:T(8,128)S(1)}, u32[]{:S(2)}, u32[]{:S(2)}) async-start(f32[4,96,512]{2,1,0:T(8,128)} %broadcast_in_dim.18), calls=%async_computation.2 | async-start | bytes 1572864 | tf_op jit(solution)/shard_map/all_to_all | solution.py:20
  77.4 14.3 %collective-permute-start = (f32[32,1024]{1,0:T(8,128)S(1)}, f32[32,1024]{1,0:T(8,128)S(1)}, u32[]{:S(2)}, u32[]{:S(2)}) collective-permute-start(f32[32,1024]{1,0:T(8,128)S(1)} %get-tuple-element.32), channel_id=1, source_target_pairs={{0,256},{32,288},{1,257},{33,289},{2,258},{34,290},{3,259},{35,291... | collective-permute-start | bytes 393224 | tf_op jit(solution)/shard_map/ppermute | solution.py:41
  85.7 10.2 %collective-permute-start.1 = (f32[32,1024]{1,0:T(8,128)S(1)}, f32[32,1024]{1,0:T(8,128)S(1)}, u32[]{:S(2)}, u32[]{:S(2)}) collective-permute-start(f32[32,1024]{1,0:T(8,128)S(1)} %get-tuple-element.31), channel_id=1, source_target_pairs={{0,288},{32,320},{1,289},{33,321},{2,290},{34,322},{3,291},{35,323... | collective-permute-start | bytes 393224 | tf_op jit(solution)/shard_map/ppermute | solution.py:41
  87.8 9.8 %collective-permute-start.10 = (f32[32,1024]{1,0:T(8,128)S(1)}, f32[32,1024]{1,0:T(8,128)S(1)}, u32[]{:S(2)}, u32[]{:S(2)}) collective-permute-start(f32[32,1024]{1,0:T(8,128)S(1)} %get-tuple-element.22), channel_id=1, source_target_pairs={{0,96},{32,128},{1,97},{33,129},{2,98},{34,130},{3,99},{35,131},{4... | collective-permute-start | bytes 393224 | tf_op jit(solution)/shard_map/ppermute | solution.py:41
  89.1 9.8 %collective-permute-start.11 = (f32[32,1024]{1,0:T(8,128)S(1)}, f32[32,1024]{1,0:T(8,128)S(1)}, u32[]{:S(2)}, u32[]{:S(2)}) collective-permute-start(f32[32,1024]{1,0:T(8,128)S(1)} %get-tuple-element.21), channel_id=1, source_target_pairs={{0,448},{32,480},{1,449},{33,481},{2,450},{34,482},{3,451},{35,483... | collective-permute-start | bytes 393224 | tf_op jit(solution)/shard_map/ppermute | solution.py:41
  90.4 14.8 %collective-permute-start.12 = (f32[32,1024]{1,0:T(8,128)S(1)}, f32[32,1024]{1,0:T(8,128)S(1)}, u32[]{:S(2)}, u32[]{:S(2)}) collective-permute-start(f32[32,1024]{1,0:T(8,128)S(1)} %get-tuple-element.20), channel_id=1, source_target_pairs={{0,64},{32,96},{1,65},{33,97},{2,66},{34,98},{3,67},{35,99},{4,68}... | collective-permute-start | bytes 393224 | tf_op jit(solution)/shard_map/ppermute | solution.py:41
  91.7 14.8 %collective-permute-start.13 = (f32[32,1024]{1,0:T(8,128)S(1)}, f32[32,1024]{1,0:T(8,128)S(1)}, u32[]{:S(2)}, u32[]{:S(2)}) collective-permute-start(f32[32,1024]{1,0:T(8,128)S(1)} %get-tuple-element.19), channel_id=1, source_target_pairs={{0,480},{32,0},{1,481},{33,1},{2,482},{34,2},{3,483},{35,3},{4,484... | collective-permute-start | bytes 393224 | tf_op jit(solution)/shard_map/ppermute | solution.py:41
  95.9 12.6 %collective-permute-start.14 = (f32[32,1024]{1,0:T(8,128)S(1)}, f32[32,1024]{1,0:T(8,128)S(1)}, u32[]{:S(2)}, u32[]{:S(2)}) collective-permute-start(f32[32,1024]{1,0:T(8,128)S(1)} %get-tuple-element.18), channel_id=1, source_target_pairs={{0,32},{32,64},{1,33},{33,65},{2,34},{34,66},{3,35},{35,67},{4,36}... | collective-permute-start | bytes 393224 | tf_op jit(solution)/shard_map/ppermute | solution.py:41
  97.6 12.9 %collective-permute-start.2 = (f32[32,1024]{1,0:T(8,128)S(1)}, f32[32,1024]{1,0:T(8,128)S(1)}, u32[]{:S(2)}, u32[]{:S(2)}) collective-permute-start(f32[32,1024]{1,0:T(8,128)S(1)} %get-tuple-element.30), channel_id=1, source_target_pairs={{0,224},{32,256},{1,225},{33,257},{2,226},{34,258},{3,227},{35,259... | collective-permute-start | bytes 393224 | tf_op jit(solution)/shard_map/ppermute | solution.py:41
  98.9 20.1 %copy-start.3 = (f32[32,1024]{1,0:T(8,128)}, f32[32,1024]{1,0:T(8,128)S(1)}, u32[]{:S(2)}) copy-start(f32[32,1024]{1,0:T(8,128)S(1)} %collective-permute-done.11) | copy-start | bytes 393220
  98.9 13.5 %collective-permute-start.3 = (f32[32,1024]{1,0:T(8,128)S(1)}, f32[32,1024]{1,0:T(8,128)S(1)}, u32[]{:S(2)}, u32[]{:S(2)}) collective-permute-start(f32[32,1024]{1,0:T(8,128)S(1)} %get-tuple-element.29), channel_id=1, source_target_pairs={{0,320},{32,352},{1,321},{33,353},{2,322},{34,354},{3,323},{35,355... | collective-permute-start | bytes 393224 | tf_op jit(solution)/shard_map/ppermute | solution.py:41
  105.2 9.1 %collective-permute-start.4 = (f32[32,1024]{1,0:T(8,128)S(1)}, f32[32,1024]{1,0:T(8,128)S(1)}, u32[]{:S(2)}, u32[]{:S(2)}) collective-permute-start(f32[32,1024]{1,0:T(8,128)S(1)} %get-tuple-element.28), channel_id=1, source_target_pairs={{0,192},{32,224},{1,193},{33,225},{2,194},{34,226},{3,195},{35,227... | collective-permute-start | bytes 393224 | tf_op jit(solution)/shard_map/ppermute | solution.py:41
  106.5 16.4 %collective-permute-start.5 = (f32[32,1024]{1,0:T(8,128)}, f32[32,1024]{1,0:T(8,128)}, u32[]{:S(2)}, u32[]{:S(2)}) collective-permute-start(f32[32,1024]{1,0:T(8,128)} %get-tuple-element.27), channel_id=1, source_target_pairs={{0,352},{32,384},{1,353},{33,385},{2,354},{34,386},{3,355},{35,387... | collective-permute-start | bytes 393224 | tf_op jit(solution)/shard_map/ppermute | solution.py:41
  108.5 14.4 %collective-permute-start.6 = (f32[32,1024]{1,0:T(8,128)}, f32[32,1024]{1,0:T(8,128)}, u32[]{:S(2)}, u32[]{:S(2)}) collective-permute-start(f32[32,1024]{1,0:T(8,128)} %get-tuple-element.26), channel_id=1, source_target_pairs={{0,160},{32,192},{1,161},{33,193},{2,162},{34,194},{3,163},{35,195... | collective-permute-start | bytes 393224 | tf_op jit(solution)/shard_map/ppermute | solution.py:41
  110.5 12.5 %collective-permute-start.7 = (f32[32,1024]{1,0:T(8,128)}, f32[32,1024]{1,0:T(8,128)}, u32[]{:S(2)}, u32[]{:S(2)}) collective-permute-start(f32[32,1024]{1,0:T(8,128)} %get-tuple-element.25), channel_id=1, source_target_pairs={{0,384},{32,416},{1,385},{33,417},{2,386},{34,418},{3,387},{35,419... | collective-permute-start | bytes 393224 | tf_op jit(solution)/shard_map/ppermute | solution.py:41
  112.4 10.5 %collective-permute-start.8 = (f32[32,1024]{1,0:T(8,128)}, f32[32,1024]{1,0:T(8,128)}, u32[]{:S(2)}, u32[]{:S(2)}) collective-permute-start(f32[32,1024]{1,0:T(8,128)} %get-tuple-element.24), channel_id=1, source_target_pairs={{0,128},{32,160},{1,129},{33,161},{2,130},{34,162},{3,131},{35,163... | collective-permute-start | bytes 393224 | tf_op jit(solution)/shard_map/ppermute | solution.py:41
  115.0 7.9 %collective-permute-start.9 = (f32[32,1024]{1,0:T(8,128)}, f32[32,1024]{1,0:T(8,128)}, u32[]{:S(2)}, u32[]{:S(2)}) collective-permute-start(f32[32,1024]{1,0:T(8,128)} %get-tuple-element.23), channel_id=1, source_target_pairs={{0,416},{32,448},{1,417},{33,449},{2,418},{34,450},{3,419},{35,451... | collective-permute-start | bytes 393224 | tf_op jit(solution)/shard_map/ppermute | solution.py:41
  119.0 25.8 %all-to-all-start.3 = ((f32[4,4,96,512]{3,2,1,0:T(8,128)}), f32[4,4,96,512]{3,2,1,0:T(8,128)S(1)}, u32[]{:S(2)}, u32[]{:S(2)}) async-start(f32[4,4,96,512]{3,2,1,0:T(8,128)} %broadcast_in_dim.19), calls=%async_computation.3 | async-start | bytes 6291456 | tf_op jit(solution)/shard_map/all_to_all | solution.py:20
  122.8 85.6 %all-gather.2.cloned.1.call-start = ((), (), s32[]{:S(2)}) async-start(), calls=%async_computation.4 | async-start | bytes 4456448 | tf_op jit(solution)/shard_map/all_gather | solution.py:154
  122.9 24.1 %copy-start.19 = (s32[2,64]{1,0:T(2,128)S(1)}, s32[2,64]{1,0:T(2,128)}, u32[]{:S(2)}) copy-start(s32[2,64]{1,0:T(2,128)} %param.9) | copy-start | bytes 1540
  122.9 25.3 %copy-start.18 = (s32[2,16]{1,0:T(2,128)S(1)}, s32[2,16]{1,0:T(2,128)}, u32[]{:S(2)}) copy-start(s32[2,16]{1,0:T(2,128)} %param.8) | copy-start | bytes 388
  144.8 8.5 %collective-permute-start.21 = (f32[16,96,512]{2,1,0:T(8,128)S(1)}, f32[16,96,512]{2,1,0:T(8,128)}, u32[]{:S(2)}, u32[]{:S(2)}) collective-permute-start(f32[16,96,512]{2,1,0:T(8,128)S(1)} %bitcast.73), channel_id=1, source_target_pairs={{0,1},{1,0},{2,3},{3,2},{4,5},{5,4},{6,7},{7,6},{8,9},{9,8},{10,11... | collective-permute-start | bytes 9437192 | tf_op jit(solution)/shard_map/ppermute | solution.py:89
  (17 other events, 59.8 us)
Sparse Core Ops, SparseCore 0:
  126.4 81.9 all-gather.1

commit v3 on v2

--- a/solution.py
+++ b/solution.py
@@ -12,10 +12,6 @@
 TILE = 8
 
 
-def matmul(a, b):
-    return jnp.dot(a, b, precision=lax.Precision.HIGH)
-
-
 def exchange(pieces, axis, groups=None):
     return lax.all_to_all(
         pieces, axis, split_axis=0, concat_axis=0, tiled=True, axis_index_groups=groups
@@ -35,12 +31,14 @@
     count, here = lax.axis_size(ROWS), lax.axis_index(ROWS)
     length = matrix.shape[0] // count
     turned = jnp.where(here == 1, jnp.roll(matrix, -length, axis=0), matrix)
-    first = second = turned[:length]
+    came = {}
     for d in send_order(count):
         pairs = [(0, d), (1, (1 + d) % count)]
-        came = lax.ppermute(turned[d * length : (d + 1) * length], ROWS, pairs)
-        first = jnp.where(here == d, came, first)
-        second = jnp.where(here == (1 + d) % count, came, second)
+        came[d] = lax.ppermute(turned[d * length : (d + 1) * length], ROWS, pairs)
+    first = second = turned[:length]
+    for d in came:
+        first = jnp.where(here == d, came[d], first)
+        second = jnp.where(here == (1 + d) % count, came[d], second)
     return jnp.concatenate([first, second], axis=0)
 
 
@@ -78,7 +76,7 @@
 
 
 def gather_plane(piece):
-    count, core = lax.axis_size(COLS), lax.axis_index(COLS) % 2
+    count = lax.axis_size(COLS)
     side, at = plane(count)
     span = range(side)
     along_x = [[[at(x, y, c) for x in span] for y in span] for c in (0, 1)]
@@ -87,8 +85,7 @@
     part = exchange(copies(part, side), COLS, along_y[0] + along_x[1])
     part = part.reshape(side * side, *piece.shape)
     other = lax.ppermute(part, COLS, [(i, i ^ 1) for i in range(count)])
-    low, high = jnp.where(core == 0, part, other), jnp.where(core == 0, other, part)
-    return jnp.concatenate([low, high], axis=0)
+    return part, other
 
 
 def halves(x):
@@ -96,27 +93,71 @@
     return high, (x - high.astype(jnp.float32)).astype(jnp.bfloat16)
 
 
-def update_kernel(steps, length, keeps, matrix, raw, left, stored, out, high, low):
-    step = pl.program_id(0)
-
-    @pl.when(step % steps == 0)
-    def _():
-        high[...], low[...] = halves(left[0])
-
+def product(left, right):
+    dot = functools.partial(jnp.dot, preferred_element_type=jnp.float32)
+    return dot(left[0], right[0]) + (dot(left[0], right[1]) + dot(left[1], right[0]))
+
+
+def factors_kernel(lines, lane, n_rows, masks, part, other, high, low, stored, inverse):
+    count, _, width = part.shape
+    wide = width // lane
+    blocks = [[] for _ in range(4)]
+    for panel in (0, 1):
+        source = jnp.where(masks[0] == panel, part[...], other[...])
+        for i, block in enumerate(blocks):
+            block.append(source[:, i * lines : (i + 1) * lines].reshape(count * lines, width))
+        for t in range(count):
+            for z in range(n_rows):
+                row = z * (width // n_rows) + (t // wide) * TILE
+                at = 4 * lines + (z // wide) * TILE
+                inverse[panel, row : row + TILE, (t % wide) * lane : (t % wide + 1) * lane] = (
+                    source[t, at : at + TILE, (z % wide) * lane : (z % wide + 1) * lane]
+                )
+    a_g0, a_g1, a_01, a_10 = (jnp.concatenate(block) for block in blocks)
+    on = [masks[i].astype(jnp.float32) for i in range(10)]
+    first = halves(inverse[0])
+    lower0 = product(halves(a_g0), first) * on[1]
+    pivot_lower = product(halves(a_10), first) * on[2]
+    a_g1 = a_g1 - product(halves(lower0), halves(a_01 * on[3]))
+    lower1 = product(halves(a_g1), halves(inverse[1])) * on[4]
+    mixed = product(halves(lower1), halves(pivot_lower))
+    stored[...] = jnp.where(masks[5] == 0, lower0, lower1)
+    for j in (0, 1):
+        high[j, :, :width], low[j, :, :width] = halves((lower0 - mixed * on[8 + j]) * on[6 + j])
+        high[j, :, width:], low[j, :, width:] = halves(lower1 * on[8 + j])
+
+
+def factors(masks, part, other, lines, lane, n_rows):
+    width = part.shape[2]
+    whole = pl.BlockSpec(memory_space=pltpu.VMEM)
+    split = jax.ShapeDtypeStruct((2, width, 2 * width), jnp.bfloat16)
+    return pl.pallas_call(
+        functools.partial(factors_kernel, lines, lane, n_rows),
+        in_specs=[pl.BlockSpec(memory_space=pltpu.SMEM), whole, whole],
+        out_specs=[whole] * 3,
+        out_shape=[split, split, jax.ShapeDtypeStruct((width, width), jnp.float32)],
+        scratch_shapes=[pltpu.VMEM((2, width, width), jnp.float32)],
+        cost_estimate=pl.CostEstimate(
+            flops=30 * width**3, bytes_accessed=8 * part.size, transcendentals=0
+        ),
+        name="factors",
+    )(masks, part, other)
+
+
+def update_kernel(steps, length, keeps, matrix, raw, high, low, stored, out):
     rows = raw.shape[0]
     starts = [*range(0, rows, 2 * length), *range(length, rows, 2 * length)]
     split = [jnp.concatenate([x[i : i + length] for i in starts]) for x in halves(raw[...])]
-    dot = functools.partial(jnp.dot, preferred_element_type=jnp.float32)
-    product = dot(high[...], split[0]) + (dot(high[...], split[1]) + dot(low[...], split[0]))
-    new = matrix[...] - product
-    out[...] = jnp.where((keeps[0] == 1) & (step < steps), stored[...], new)
-
-
-def update(keeps, matrix, raw, left, stored, length):
+    new = matrix[...] - product((high[0], low[0]), split)
+    out[...] = jnp.where((keeps[0] == 1) & (pl.program_id(0) < steps), stored[...], new)
+
+
+def update(keeps, matrix, raw, high, low, stored, length):
     rows, width = stored.shape
     cols = matrix.shape[1]
     wide = min(256, width)
     steps = width // wide
+    factor = pl.BlockSpec((1, rows, 2 * rows), lambda t, _: (t // steps, 0, 0))
     return pl.pallas_call(
         functools.partial(update_kernel, steps, length),
         grid_spec=pltpu.PrefetchScalarGridSpec(
@@ -125,18 +166,18 @@
             in_specs=[
                 pl.BlockSpec((rows, wide), lambda t, _: (0, t)),
                 pl.BlockSpec((2 * rows, wide), lambda t, _: (0, t)),
-                pl.BlockSpec((1, rows, 2 * rows), lambda t, _: (t // steps, 0, 0)),
+                factor,
+                factor,
                 pl.BlockSpec((rows, wide), lambda t, _: (0, jnp.minimum(t, steps - 1))),
             ],
             out_specs=pl.BlockSpec((rows, wide), lambda t, _: (0, t)),
-            scratch_shapes=[pltpu.VMEM((rows, 2 * rows), jnp.bfloat16)] * 2,
         ),
         out_shape=jax.ShapeDtypeStruct(matrix.shape, jnp.float32),
         cost_estimate=pl.CostEstimate(
             flops=12 * rows * rows * cols, bytes_accessed=32 * rows * cols, transcendentals=0
         ),
         name="update",
-    )(keeps, matrix, raw, left, stored)
+    )(keeps, matrix, raw, high, low, stored)
 
 
 def per_device(matrix, pivot_inverse, row_live, col_live):
@@ -163,41 +204,21 @@
     pivots = pivots.transpose(0, 2, 1, 3).reshape(-1, width)
 
     piece = jnp.concatenate([*mine, *cross, pivots], axis=0)
-    shared = gather_plane(piece)
-    a_g0, a_g1, a_01, a_10 = (
-        shared[:, i * lines : (i + 1) * lines].reshape(width, width) for i in range(4)
-    )
-    inverse = shared[:, 4 * lines :].reshape(
-        2, row_groups, col_groups, n_rows // wide, TILE, wide, lane
-    )
-    inverse = inverse.transpose(0, 3, 5, 1, 4, 2, 6).reshape(2, width, width)
+    part, other = gather_plane(piece)
 
     def lower(panel, row):
-        return jnp.where(row > panel, row_live[panel, row], 0).astype(jnp.float32)
+        return jnp.where(row > panel, row_live[panel, row], 0)
 
     col_index = jnp.arange(matrix.shape[1] // width, dtype=jnp.int32) * n_cols + p
 
     def upper(panel):
-        live = jnp.where(col_index > panel, jnp.take(col_live[panel], col_index), 0)
-        return live.astype(jnp.float32)
-
-    up0, up1 = upper(0), upper(1)
-    both = matmul(jnp.concatenate([a_g0, a_10], axis=0), inverse[0])
-    lower0 = both[:width] * lower(0, g)
-    pivot_lower = both[width:] * lower(0, jnp.int32(1))
-    a_g1 = a_g1 - matmul(lower0, a_01 * col_live[0, 1].astype(jnp.float32))
-    lower1 = matmul(a_g1, inverse[1]) * lower(1, g)
-    mixed = matmul(lower1, pivot_lower)
-
-    left = jnp.stack(
-        [
-            jnp.concatenate([(lower0 - mixed * up1[j]) * up0[j], lower1 * up1[j]], axis=1)
-            for j in range(matrix.shape[1] // width)
-        ]
-    )
-    stored = jnp.where(p == 0, lower0, lower1)
+        return jnp.where(col_index > panel, jnp.take(col_live[panel], col_index), 0)
+
+    scalars = jnp.stack([p % 2, lower(0, g), lower(0, jnp.int32(1)), col_live[0, 1], lower(1, g), p])
+    masks = jnp.concatenate([scalars, upper(0), upper(1)])
+    high, low, stored = factors(masks, part, other, lines=lines, lane=lane, n_rows=n_rows)
     keeps = jnp.where(p == 0, g > 0, (p == 1) & (g > 1)).astype(jnp.int32).reshape(1)
-    return update(keeps, matrix, raw, left, stored, length=width // n_rows)
+    return update(keeps, matrix, raw, high, low, stored, length=width // n_rows)
 
 
 def solution(mesh):

time: 226 us -> 181 us (0.80)
  the two profiles are of different devices: /device:TPU:6 before, /device:TPU:1 now
where the time goes in v3:
time: 181 us; the launch traced here: 180 us
  starting transfers between devices  74.9 us (41%)
  blocking collectives  37.4 us (21%)
  Pallas kernels  18.8 us (10%)
  waiting for transfers between devices  18.5 us (10%)
  between operations  15.2 us (8%)
  local copies, waits for them, and re-layouts  10.1 us (6%)
  other arithmetic  5.07 us (3%)
    all_to_all x2, blocking collectives, exchange(): lax.all_to_all(pieces, axis, split_axis=0, concat_axis=0, tiled=True, axi...  37.4 us
    ppermute x15, starting transfers between devices, scatter_rows(): came[d] = lax.ppermute(turned[d * length:(d + 1) * length], ROWS, pairs)  36.8 us
    ppermute x15, waiting for transfers between devices, scatter_rows(): came[d] = lax.ppermute(turned[d * length:(d + 1) * length], ROWS, pairs)  15.3 us
    all_to_all x2, starting transfers between devices, exchange(): lax.all_to_all(pieces, axis, split_axis=0, concat_axis=0, tiled=True, axi...  14.5 us
    pallas_call x1, Pallas kernels, factors(): pl.pallas_call(functools.partial(factors_kernel, lines, lane, n_rows), in...  10.3 us
    ppermute x3, starting transfers between devices, tree_copies(): leaves.append(lax.ppermute(held, ROWS, pairs))  8.5 us
    pallas_call x1, Pallas kernels, update(): pl.pallas_call(functools.partial(update_kernel, steps, length), grid_spec...  8.43 us
    ppermute x3, starting transfers between devices, tree_copies(): came = lax.ppermute(own, ROWS, [(0, c), (1, c + 1)])  7.8 us
  transfers between devices with their start and end apart: 25, of which 7 were waited for; matrix products, arithmetic and copies ran while one was open for 6% of the time, Pallas kernels for 6%

profile of v3, /device:TPU:1, one launch (start us, length us, event | category | flops | bytes accessed | tf_op | source)
XLA Modules:
  0.0 180.0 jit_solution(3248839745931856319)
XLA Ops:
  6.5 1.5 slice-done
  8.1 2.0 %maximum_select_fusion = f32[512,1024]{1,0:T(8,128)S(1)} fusion(f32[512,1024]{1,0:T(8,128)} %matrix.1, f32[32,1024]{1,0:T(8,128)S(1)} %slice-done.1, f32[480,1024]{1,0:T(8,128)S(1)} %slice-done, pred[]{:T(512)S(6)} %eq.105), kind=kLoop, calls=%fused_computation.2 | loop fusion | flops 1048576 | bytes 6291457 | tf_op jit(solution)/shard_map/jit(_where)/select_n | solution.py:33
  11.0 16.4 %collective-permute-start = (f32[32,1024]{1,0:T(8,128)S(1)}, f32[32,1024]{1,0:T(8,128)S(1)}, u32[]{:S(2)}, u32[]{:S(2)}) collective-permute-start(f32[32,1024]{1,0:T(8,128)S(1)} %get-tuple-element.28), channel_id=1, source_target_pairs={{0,256},{32,288},{1,257},{33,289},{2,258},{34,290},{3,259},{35,291... | collective-permute-start | bytes 393224 | tf_op jit(solution)/shard_map/ppermute | solution.py:37
  27.4 1.3 collective-permute-start.1
  28.7 1.3 collective-permute-start.10
  30.0 1.3 collective-permute-start.11
  31.3 1.3 collective-permute-start.12
  32.7 1.9 %collective-permute-start.13 = (f32[32,1024]{1,0:T(8,128)}, f32[32,1024]{1,0:T(8,128)S(1)}, u32[]{:S(2)}, u32[]{:S(2)}) collective-permute-start(f32[32,1024]{1,0:T(8,128)} %get-tuple-element.15), channel_id=1, source_target_pairs={{0,480},{32,0},{1,481},{33,1},{2,482},{34,2},{3,483},{35,3},{4,484... | collective-permute-start | bytes 393224 | tf_op jit(solution)/shard_map/ppermute | solution.py:37
  34.6 4.8 %collective-permute-done.1 = f32[32,1024]{1,0:T(8,128)S(1)} collective-permute-done((f32[32,1024]{1,0:T(8,128)S(1)}, f32[32,1024]{1,0:T(8,128)S(1)}, u32[]{:S(2)}, u32[]{:S(2)}) %collective-permute-start.1) | collective-permute-done | bytes 131104 | tf_op jit(solution)/shard_map/ppermute | solution.py:37
  40.7 1.3 collective-permute-start.2
  42.2 3.0 %collective-permute-start.3 = (f32[32,1024]{1,0:T(8,128)S(1)}, f32[32,1024]{1,0:T(8,128)S(1)}, u32[]{:S(2)}, u32[]{:S(2)}) collective-permute-start(f32[32,1024]{1,0:T(8,128)S(1)} %get-tuple-element.25), channel_id=1, source_target_pairs={{0,320},{32,352},{1,321},{33,353},{2,322},{34,354},{3,323},{35,355... | collective-permute-start | bytes 393224 | tf_op jit(solution)/shard_map/ppermute | solution.py:37
  45.2 1.3 collective-permute-start.4
  47.8 10.1 %all-to-all-start = ((f32[32,16,512]{2,1,0:T(8,128)}), f32[32,16,512]{2,1,0:T(8,128)S(1)}, u32[]{:S(2)}, u32[]{:S(2)}) async-start(f32[32,16,512]{2,1,0:T(8,128)} %bitcast.15), calls=%async_computation | async-start | bytes 2097152 | tf_op jit(solution)/shard_map/all_to_all | solution.py:16
  57.9 1.3 collective-permute-start.5
  59.2 1.3 collective-permute-start.6
  60.5 1.3 collective-permute-start.7
  61.9 1.3 collective-permute-start.8
  63.2 1.3 collective-permute-start.9
  65.4 4.7 %collective-permute-done.5 = f32[32,1024]{1,0:T(8,128)S(1)} collective-permute-done((f32[32,1024]{1,0:T(8,128)}, f32[32,1024]{1,0:T(8,128)S(1)}, u32[]{:S(2)}, u32[]{:S(2)}) %collective-permute-start.5) | collective-permute-done | bytes 131104 | tf_op jit(solution)/shard_map/ppermute | solution.py:37
  70.1 2.7 %collective-permute-done.7 = f32[32,1024]{1,0:T(8,128)S(1)} collective-permute-done((f32[32,1024]{1,0:T(8,128)S(1)}, f32[32,1024]{1,0:T(8,128)S(1)}, u32[]{:S(2)}, u32[]{:S(2)}) %collective-permute-start.7) | collective-permute-done | bytes 131104 | tf_op jit(solution)/shard_map/ppermute | solution.py:37
  72.8 2.8 %collective-permute-done.9 = f32[32,1024]{1,0:T(8,128)S(1)} collective-permute-done((f32[32,1024]{1,0:T(8,128)S(1)}, f32[32,1024]{1,0:T(8,128)S(1)}, u32[]{:S(2)}, u32[]{:S(2)}) %collective-permute-start.9) | collective-permute-done | bytes 131104 | tf_op jit(solution)/shard_map/ppermute | solution.py:37
  78.6 5.2 %collective-permute-start.15 = (f32[16,512]{1,0:T(8,128)S(1)}, f32[16,512]{1,0:T(8,128)S(1)}, u32[]{:S(2)}, u32[]{:S(2)}) collective-permute-start(f32[16,512]{1,0:T(8,128)S(1)} %get-tuple-element.29), channel_id=1, source_target_pairs={{0,384},{32,416},{1,385},{33,417},{2,386},{34,418},{3,387},{35,419... | collective-permute-start | bytes 98312 | tf_op jit(solution)/shard_map/ppermute | solution.py:49
  87.1 4.5 %all-to-all-start.1 = ((f32[16,8,128]{2,1,0:T(8,128)}), f32[16,8,128]{2,1,0:T(8,128)S(1)}, u32[]{:S(2)}, u32[]{:S(2)}) async-start(f32[16,8,128]{2,1,0:T(8,128)} %broadcast_in_dim.15), calls=%async_computation.1 | async-start | bytes 131072 | tf_op jit(solution)/shard_map/all_to_all | solution.py:16
  91.6 4.4 %collective-permute-start.18 = (f32[16,512]{1,0:T(8,128)S(1)}, f32[16,512]{1,0:T(8,128)S(1)}, u32[]{:S(2)}, u32[]{:S(2)}) collective-permute-start(f32[16,512]{1,0:T(8,128)S(1)} %select_select_fusion.2), channel_id=1, source_target_pairs={{0,480},{32,0},{128,96},{160,128},{256,224},{288,256},{384,352},{4... | collective-permute-start | bytes 98312 | tf_op jit(solution)/shard_map/ppermute | solution.py:54
  97.4 2.8 %collective-permute-start.20 = (f32[16,512]{1,0:T(8,128)S(1)}, f32[16,512]{1,0:T(8,128)S(1)}, u32[]{:S(2)}, u32[]{:S(2)}) collective-permute-start(f32[16,512]{1,0:T(8,128)S(1)} %select_select_fusion.2), channel_id=1, source_target_pairs={{0,32},{32,64},{128,160},{160,192},{256,288},{288,320},{384,416},{... | collective-permute-start | bytes 98312 | tf_op jit(solution)/shard_map/ppermute | solution.py:54
  101.4 2.0 %all-to-all-done.1 = f32[16,8,128]{2,1,0:T(8,128)S(1)} async-done(((f32[16,8,128]{2,1,0:T(8,128)}), f32[16,8,128]{2,1,0:T(8,128)S(1)}, u32[]{:S(2)}, u32[]{:S(2)}) %all-to-all-start.1) | async-done | bytes 65568 | tf_op jit(solution)/shard_map/all_to_all | solution.py:16
  103.5 12.5 %all_to_all.20 = f32[4,96,512]{2,1,0:T(8,128)S(1)} all-to-all(f32[4,96,512]{2,1,0:T(8,128)S(1)} %broadcast_in_dim.16), channel_id=1, replica_groups={{0,8,16,24},{2,10,18,26},{4,12,20,28},{6,14,22,30},{1,3,5,7},{9,11,13,1..., dimensions={0} | all-to-all | bytes 1572864 | tf_op jit(solution)/shard_map/all_to_all | solution.py:16
  116.5 24.9 %all_to_all.21 = f32[4,4,96,512]{3,2,1,0:T(8,128)S(1)} all-to-all(f32[4,4,96,512]{3,2,1,0:T(8,128)S(1)} %broadcast_in_dim.17), channel_id=1, replica_groups={{0,2,4,6},{8,10,12,14},{16,18,20,22},{24,26,28,30},{1,9,17,25},{3,11,19..., dimensions={0} | all-to-all | bytes 6291456 | tf_op jit(solution)/shard_map/all_to_all | solution.py:16
  141.4 7.2 %collective-permute-start.21 = (f32[16,96,512]{2,1,0:T(8,128)S(1)}, f32[16,96,512]{2,1,0:T(8,128)}, u32[]{:S(2)}, u32[]{:S(2)}) collective-permute-start(f32[16,96,512]{2,1,0:T(8,128)S(1)} %bitcast.52), channel_id=1, source_target_pairs={{0,1},{1,0},{2,3},{3,2},{4,5},{5,4},{6,7},{7,6},{8,9},{9,8},{10,11... | collective-permute-start | bytes 9437192 | tf_op jit(solution)/shard_map/ppermute | solution.py:87
  152.4 2.0 %concatenate.15.masks = s32[10]{0:T(128)} concatenate(s32[1]{0:T(128)} %bitcast.1, s32[1]{0:T(128)} %bitcast.3, s32[1]{0:T(128)} %bitcast.4, s32[1]{0:T(128)} %bitcast.5, s32[1]{0:T(128)} %bitcast.7, s32[1]{0:T(128)} %bitcast.8, s32[2]{0:T(128)S(1)} %get-tuple-element.39, s32[2]{0:T(128)S(1)} %get-tuple-element.38), dimensions={0} | concatenate | bytes 80 | tf_op jit(solution)/shard_map/concatenate | solution.py:218
  154.4 10.3 %factors.1 = (bf16[2,512,1024]{2,1,0:T(8,128)(2,1)}, bf16[2,512,1024]{2,1,0:T(8,128)(2,1)}, f32[512,512]{1,0:T(8,128)}) custom-call(s32[10]{0:T(128)} %concatenate.15.masks, f32[16,96,512]{2,1,0:T(8,128)} %bitcast.53, f32[16,96,512]{2,1,0:T(8,128)} %collective-permute-done.21.other), custom_call_target="tpu_custom_call" | custom-call | flops 4026531840 | bytes 6291456 | tf_op jit(solution)/shard_map/factors/pallas_call | solution.py:134
  164.7 8.4 %update.1 = f32[512,1024]{1,0:T(8,128)} custom-call(s32[1]{0:T(128)} %bitcast.keeps, f32[512,1024]{1,0:T(8,128)} %matrix.1, f32[1024,1024]{1,0:T(8,128)} %all-gather.2.cloned.1.call-done.raw, bf16[2,512,1024]{2,1,0:T(8,128)(2,1)} %get-tuple-element.9.high, bf16[2,512,1024]{2,1,0:T(8,128)(2,1)} %get-tuple-element.10.low, f32[512,512]{1,0:T(8,128)} %get-tuple-element.11.stored), custom_call_target="tpu_custom_call" | custom-call | flops 3221225472 | bytes 16777216 | tf_op jit(solution)/shard_map/update/pallas_call | solution.py:161
  (66 shorter events, 16.3 us)
Async XLA Ops:
  6.5 1.5 slice-start
  6.5 1.5 slice-start.1
  10.1 22.6 %copy-start.1 = (f32[512,1024]{1,0:T(8,128)}, f32[512,1024]{1,0:T(8,128)S(1)}, u32[]{:S(2)}) copy-start(f32[512,1024]{1,0:T(8,128)S(1)} %maximum_select_fusion) | copy-start | bytes 6291460
  10.1 22.5 %copy-start = (f32[512,1024]{1,0:T(8,128)S(1)}, f32[512,1024]{1,0:T(8,128)}, u32[]{:S(2)}) copy-start(f32[512,1024]{1,0:T(8,128)} %matrix.1) | copy-start | bytes 6291460
  11.0 21.7 %collective-permute-start = (f32[32,1024]{1,0:T(8,128)S(1)}, f32[32,1024]{1,0:T(8,128)S(1)}, u32[]{:S(2)}, u32[]{:S(2)}) collective-permute-start(f32[32,1024]{1,0:T(8,128)S(1)} %get-tuple-element.28), channel_id=1, source_target_pairs={{0,256},{32,288},{1,257},{33,289},{2,258},{34,290},{3,259},{35,291... | collective-permute-start | bytes 393224 | tf_op jit(solution)/shard_map/ppermute | solution.py:37
  27.4 12.1 %collective-permute-start.1 = (f32[32,1024]{1,0:T(8,128)S(1)}, f32[32,1024]{1,0:T(8,128)S(1)}, u32[]{:S(2)}, u32[]{:S(2)}) collective-permute-start(f32[32,1024]{1,0:T(8,128)S(1)} %get-tuple-element.27), channel_id=1, source_target_pairs={{0,288},{32,320},{1,289},{33,321},{2,290},{34,322},{3,291},{35,323... | collective-permute-start | bytes 393224 | tf_op jit(solution)/shard_map/ppermute | solution.py:37
  28.7 12.1 %collective-permute-start.10 = (f32[32,1024]{1,0:T(8,128)S(1)}, f32[32,1024]{1,0:T(8,128)S(1)}, u32[]{:S(2)}, u32[]{:S(2)}) collective-permute-start(f32[32,1024]{1,0:T(8,128)S(1)} %get-tuple-element.18), channel_id=1, source_target_pairs={{0,96},{32,128},{1,97},{33,129},{2,98},{34,130},{3,99},{35,131},{4... | collective-permute-start | bytes 393224 | tf_op jit(solution)/shard_map/ppermute | solution.py:37
  30.0 12.3 %collective-permute-start.11 = (f32[32,1024]{1,0:T(8,128)S(1)}, f32[32,1024]{1,0:T(8,128)S(1)}, u32[]{:S(2)}, u32[]{:S(2)}) collective-permute-start(f32[32,1024]{1,0:T(8,128)S(1)} %get-tuple-element.17), channel_id=1, source_target_pairs={{0,448},{32,480},{1,449},{33,481},{2,450},{34,482},{3,451},{35,483... | collective-permute-start | bytes 393224 | tf_op jit(solution)/shard_map/ppermute | solution.py:37
  31.3 13.9 %collective-permute-start.12 = (f32[32,1024]{1,0:T(8,128)S(1)}, f32[32,1024]{1,0:T(8,128)S(1)}, u32[]{:S(2)}, u32[]{:S(2)}) collective-permute-start(f32[32,1024]{1,0:T(8,128)S(1)} %get-tuple-element.16), channel_id=1, source_target_pairs={{0,64},{32,96},{1,65},{33,97},{2,66},{34,98},{3,67},{35,99},{4,68}... | collective-permute-start | bytes 393224 | tf_op jit(solution)/shard_map/ppermute | solution.py:37
  32.7 25.2 %collective-permute-start.13 = (f32[32,1024]{1,0:T(8,128)}, f32[32,1024]{1,0:T(8,128)S(1)}, u32[]{:S(2)}, u32[]{:S(2)}) collective-permute-start(f32[32,1024]{1,0:T(8,128)} %get-tuple-element.15), channel_id=1, source_target_pairs={{0,480},{32,0},{1,481},{33,1},{2,482},{34,2},{3,483},{35,3},{4,484... | collective-permute-start | bytes 393224 | tf_op jit(solution)/shard_map/ppermute | solution.py:37
  39.4 19.8 %collective-permute-start.14 = (f32[32,1024]{1,0:T(8,128)}, f32[32,1024]{1,0:T(8,128)S(1)}, u32[]{:S(2)}, u32[]{:S(2)}) collective-permute-start(f32[32,1024]{1,0:T(8,128)} %get-tuple-element.14), channel_id=1, source_target_pairs={{0,32},{32,64},{1,33},{33,65},{2,34},{34,66},{3,35},{35,67},{4,36}... | collective-permute-start | bytes 393224 | tf_op jit(solution)/shard_map/ppermute | solution.py:37
  40.7 19.8 %collective-permute-start.2 = (f32[32,1024]{1,0:T(8,128)S(1)}, f32[32,1024]{1,0:T(8,128)S(1)}, u32[]{:S(2)}, u32[]{:S(2)}) collective-permute-start(f32[32,1024]{1,0:T(8,128)S(1)} %get-tuple-element.26), channel_id=1, source_target_pairs={{0,224},{32,256},{1,225},{33,257},{2,226},{34,258},{3,227},{35,259... | collective-permute-start | bytes 393224 | tf_op jit(solution)/shard_map/ppermute | solution.py:37
  42.2 19.6 %collective-permute-start.3 = (f32[32,1024]{1,0:T(8,128)S(1)}, f32[32,1024]{1,0:T(8,128)S(1)}, u32[]{:S(2)}, u32[]{:S(2)}) collective-permute-start(f32[32,1024]{1,0:T(8,128)S(1)} %get-tuple-element.25), channel_id=1, source_target_pairs={{0,320},{32,352},{1,321},{33,353},{2,322},{34,354},{3,323},{35,355... | collective-permute-start | bytes 393224 | tf_op jit(solution)/shard_map/ppermute | solution.py:37
  45.2 17.9 %collective-permute-start.4 = (f32[32,1024]{1,0:T(8,128)S(1)}, f32[32,1024]{1,0:T(8,128)S(1)}, u32[]{:S(2)}, u32[]{:S(2)}) collective-permute-start(f32[32,1024]{1,0:T(8,128)S(1)} %get-tuple-element.24), channel_id=1, source_target_pairs={{0,192},{32,224},{1,193},{33,225},{2,194},{34,226},{3,195},{35,227... | collective-permute-start | bytes 393224 | tf_op jit(solution)/shard_map/ppermute | solution.py:37
  47.8 30.8 %all-to-all-start = ((f32[32,16,512]{2,1,0:T(8,128)}), f32[32,16,512]{2,1,0:T(8,128)S(1)}, u32[]{:S(2)}, u32[]{:S(2)}) async-start(f32[32,16,512]{2,1,0:T(8,128)} %bitcast.15), calls=%async_computation | async-start | bytes 2097152 | tf_op jit(solution)/shard_map/all_to_all | solution.py:16
  57.8 106.9 %all-gather.2.cloned.1.call-start = ((), (), s32[]{:S(2)}) async-start(), calls=%async_computation.4 | async-start | bytes 4456448 | tf_op jit(solution)/shard_map/all_gather | solution.py:195
  57.9 12.2 %collective-permute-start.5 = (f32[32,1024]{1,0:T(8,128)}, f32[32,1024]{1,0:T(8,128)S(1)}, u32[]{:S(2)}, u32[]{:S(2)}) collective-permute-start(f32[32,1024]{1,0:T(8,128)} %get-tuple-element.23), channel_id=1, source_target_pairs={{0,352},{32,384},{1,353},{33,385},{2,354},{34,386},{3,355},{35,387... | collective-permute-start | bytes 393224 | tf_op jit(solution)/shard_map/ppermute | solution.py:37
  59.2 10.9 %collective-permute-start.6 = (f32[32,1024]{1,0:T(8,128)}, f32[32,1024]{1,0:T(8,128)S(1)}, u32[]{:S(2)}, u32[]{:S(2)}) collective-permute-start(f32[32,1024]{1,0:T(8,128)} %get-tuple-element.22), channel_id=1, source_target_pairs={{0,160},{32,192},{1,161},{33,193},{2,162},{34,194},{3,163},{35,195... | collective-permute-start | bytes 393224 | tf_op jit(solution)/shard_map/ppermute | solution.py:37
  60.5 12.3 %collective-permute-start.7 = (f32[32,1024]{1,0:T(8,128)S(1)}, f32[32,1024]{1,0:T(8,128)S(1)}, u32[]{:S(2)}, u32[]{:S(2)}) collective-permute-start(f32[32,1024]{1,0:T(8,128)S(1)} %get-tuple-element.21), channel_id=1, source_target_pairs={{0,384},{32,416},{1,385},{33,417},{2,386},{34,418},{3,387},{35,419... | collective-permute-start | bytes 393224 | tf_op jit(solution)/shard_map/ppermute | solution.py:37
  61.9 11.0 %collective-permute-start.8 = (f32[32,1024]{1,0:T(8,128)S(1)}, f32[32,1024]{1,0:T(8,128)S(1)}, u32[]{:S(2)}, u32[]{:S(2)}) collective-permute-start(f32[32,1024]{1,0:T(8,128)S(1)} %get-tuple-element.20), channel_id=1, source_target_pairs={{0,128},{32,160},{1,129},{33,161},{2,130},{34,162},{3,131},{35,163... | collective-permute-start | bytes 393224 | tf_op jit(solution)/shard_map/ppermute | solution.py:37
  63.2 12.5 %collective-permute-start.9 = (f32[32,1024]{1,0:T(8,128)S(1)}, f32[32,1024]{1,0:T(8,128)S(1)}, u32[]{:S(2)}, u32[]{:S(2)}) collective-permute-start(f32[32,1024]{1,0:T(8,128)S(1)} %get-tuple-element.19), channel_id=1, source_target_pairs={{0,416},{32,448},{1,417},{33,449},{2,418},{34,450},{3,419},{35,451... | collective-permute-start | bytes 393224 | tf_op jit(solution)/shard_map/ppermute | solution.py:37
  78.6 13.0 %collective-permute-start.15 = (f32[16,512]{1,0:T(8,128)S(1)}, f32[16,512]{1,0:T(8,128)S(1)}, u32[]{:S(2)}, u32[]{:S(2)}) collective-permute-start(f32[16,512]{1,0:T(8,128)S(1)} %get-tuple-element.29), channel_id=1, source_target_pairs={{0,384},{32,416},{1,385},{33,417},{2,386},{34,418},{3,387},{35,419... | collective-permute-start | bytes 98312 | tf_op jit(solution)/shard_map/ppermute | solution.py:49
  83.8 7.8 %collective-permute-start.16 = (f32[16,512]{1,0:T(8,128)S(1)}, f32[16,512]{1,0:T(8,128)S(1)}, u32[]{:S(2)}, u32[]{:S(2)}) collective-permute-start(f32[16,512]{1,0:T(8,128)S(1)} %get-tuple-element.29), channel_id=1, source_target_pairs={{0,256},{32,288},{1,257},{33,289},{2,258},{34,290},{3,259},{35,291... | collective-permute-start | bytes 98312 | tf_op jit(solution)/shard_map/ppermute | solution.py:49
  85.1 6.5 %collective-permute-start.17 = (f32[16,512]{1,0:T(8,128)S(1)}, f32[16,512]{1,0:T(8,128)S(1)}, u32[]{:S(2)}, u32[]{:S(2)}) collective-permute-start(f32[16,512]{1,0:T(8,128)S(1)} %get-tuple-element.29), channel_id=1, source_target_pairs={{0,128},{32,160},{1,129},{33,161},{2,130},{34,162},{3,131},{35,163... | collective-permute-start | bytes 98312 | tf_op jit(solution)/shard_map/ppermute | solution.py:49
  87.1 16.3 %all-to-all-start.1 = ((f32[16,8,128]{2,1,0:T(8,128)}), f32[16,8,128]{2,1,0:T(8,128)S(1)}, u32[]{:S(2)}, u32[]{:S(2)}) async-start(f32[16,8,128]{2,1,0:T(8,128)} %broadcast_in_dim.15), calls=%async_computation.1 | async-start | bytes 131072 | tf_op jit(solution)/shard_map/all_to_all | solution.py:16
  91.6 8.5 %collective-permute-start.18 = (f32[16,512]{1,0:T(8,128)S(1)}, f32[16,512]{1,0:T(8,128)S(1)}, u32[]{:S(2)}, u32[]{:S(2)}) collective-permute-start(f32[16,512]{1,0:T(8,128)S(1)} %select_select_fusion.2), channel_id=1, source_target_pairs={{0,480},{32,0},{128,96},{160,128},{256,224},{288,256},{384,352},{4... | collective-permute-start | bytes 98312 | tf_op jit(solution)/shard_map/ppermute | solution.py:54
  96.1 4.1 %collective-permute-start.19 = (f32[16,512]{1,0:T(8,128)S(1)}, f32[16,512]{1,0:T(8,128)S(1)}, u32[]{:S(2)}, u32[]{:S(2)}) collective-permute-start(f32[16,512]{1,0:T(8,128)S(1)} %select_select_fusion.2), channel_id=1, source_target_pairs={{0,64},{32,96},{128,192},{160,224},{256,320},{288,352},{384,448},{... | collective-permute-start | bytes 98312 | tf_op jit(solution)/shard_map/ppermute | solution.py:54
  97.4 4.0 %collective-permute-start.20 = (f32[16,512]{1,0:T(8,128)S(1)}, f32[16,512]{1,0:T(8,128)S(1)}, u32[]{:S(2)}, u32[]{:S(2)}) collective-permute-start(f32[16,512]{1,0:T(8,128)S(1)} %select_select_fusion.2), channel_id=1, source_target_pairs={{0,32},{32,64},{128,160},{160,192},{256,288},{288,320},{384,416},{... | collective-permute-start | bytes 98312 | tf_op jit(solution)/shard_map/ppermute | solution.py:54
  116.4 32.2 %copy-start.4 = (s32[2,64]{1,0:T(2,128)S(1)}, s32[2,64]{1,0:T(2,128)}, u32[]{:S(2)}) copy-start(s32[2,64]{1,0:T(2,128)} %param.9) | copy-start | bytes 1540
  116.5 34.1 %copy-start.3 = (s32[2,16]{1,0:T(2,128)S(1)}, s32[2,16]{1,0:T(2,128)}, u32[]{:S(2)}) copy-start(s32[2,16]{1,0:T(2,128)} %param.8) | copy-start | bytes 388
  141.4 13.0 %copy-start.2 = (f32[4,4,96,512]{3,2,1,0:T(8,128)}, f32[4,4,96,512]{3,2,1,0:T(8,128)S(1)}, u32[]{:S(2)}) copy-start(f32[4,4,96,512]{3,2,1,0:T(8,128)S(1)} %all_to_all.21) | copy-start | bytes 9437188
  141.4 13.0 %collective-permute-start.21 = (f32[16,96,512]{2,1,0:T(8,128)S(1)}, f32[16,96,512]{2,1,0:T(8,128)}, u32[]{:S(2)}, u32[]{:S(2)}) collective-permute-start(f32[16,96,512]{2,1,0:T(8,128)S(1)} %bitcast.52), channel_id=1, source_target_pairs={{0,1},{1,0},{2,3},{3,2},{4,5},{5,4},{6,7},{7,6},{8,9},{9,8},{10,11... | collective-permute-start | bytes 9437192 | tf_op jit(solution)/shard_map/ppermute | solution.py:87
Sparse Core Ops, SparseCore 0:
  78.7 69.3 all-gather.1

commit v4 on v3

--- a/solution.py
+++ b/solution.py
@@ -27,19 +27,40 @@
     return [*half, count // 2]
 
 
+def pick_kernel(length, *refs):
+    *came, out, semaphores = refs
+    count, here = len(came), lax.axis_index(ROWS)
+    for panel in (0, 1):
+        part = out.at[pl.ds(panel * length, length)]
+        for d, source in enumerate(came):
+            @pl.when(lax.rem(here + count - panel, count) == d)
+            def _():
+                pltpu.make_async_copy(source, part, semaphores.at[panel]).start()
+    for panel in (0, 1):
+        part = out.at[pl.ds(panel * length, length)]
+        pltpu.make_async_copy(came[0], part, semaphores.at[panel]).wait()
+
+
 def scatter_rows(matrix):
     count, here = lax.axis_size(ROWS), lax.axis_index(ROWS)
-    length = matrix.shape[0] // count
+    length, cols = matrix.shape[0] // count, matrix.shape[1]
     turned = jnp.where(here == 1, jnp.roll(matrix, -length, axis=0), matrix)
-    came = {}
+    came = [turned[d * length : (d + 1) * length] for d in range(count)]
     for d in send_order(count):
         pairs = [(0, d), (1, (1 + d) % count)]
-        came[d] = lax.ppermute(turned[d * length : (d + 1) * length], ROWS, pairs)
-    first = second = turned[:length]
-    for d in came:
-        first = jnp.where(here == d, came[d], first)
-        second = jnp.where(here == (1 + d) % count, came[d], second)
-    return jnp.concatenate([first, second], axis=0)
+        came[d] = lax.ppermute(came[d], ROWS, pairs)
+    return pl.pallas_call(
+        functools.partial(pick_kernel, length),
+        in_specs=[pl.BlockSpec(memory_space=pl.ANY)] * count,
+        out_specs=pl.BlockSpec(memory_space=pltpu.VMEM),
+        out_shape=jax.ShapeDtypeStruct((2 * length, cols), jnp.float32),
+        scratch_shapes=[pltpu.SemaphoreType.DMA((2,))],
+        cost_estimate=pl.CostEstimate(
+            flops=matrix.size, bytes_accessed=16 * length * cols, transcendentals=0
+        ),
+        compiler_params=pltpu.CompilerParams(vmem_limit_bytes=4 * 2**20),
+        name="pick",
+    )(*came)
 
 
 def tree_copies(own):
@@ -140,6 +161,7 @@
         cost_estimate=pl.CostEstimate(
             flops=30 * width**3, bytes_accessed=8 * part.size, transcendentals=0
         ),
+        compiler_params=pltpu.CompilerParams(vmem_limit_bytes=36 * 2**20),
         name="factors",
     )(masks, part, other)
 
@@ -148,7 +170,8 @@
     rows = raw.shape[0]
     starts = [*range(0, rows, 2 * length), *range(length, rows, 2 * length)]
     split = [jnp.concatenate([x[i : i + length] for i in starts]) for x in halves(raw[...])]
-    new = matrix[...] - product((high[0], low[0]), split)
+    block = pl.program_id(0) // steps
+    new = matrix[...] - product((high[block], low[block]), split)
     out[...] = jnp.where((keeps[0] == 1) & (pl.program_id(0) < steps), stored[...], new)
 
 
@@ -157,7 +180,7 @@
     cols = matrix.shape[1]
     wide = min(256, width)
     steps = width // wide
-    factor = pl.BlockSpec((1, rows, 2 * rows), lambda t, _: (t // steps, 0, 0))
+    factor = pl.BlockSpec(memory_space=pltpu.VMEM)
     return pl.pallas_call(
         functools.partial(update_kernel, steps, length),
         grid_spec=pltpu.PrefetchScalarGridSpec(
@@ -176,6 +199,7 @@
         cost_estimate=pl.CostEstimate(
             flops=12 * rows * rows * cols, bytes_accessed=32 * rows * cols, transcendentals=0
         ),
+        compiler_params=pltpu.CompilerParams(vmem_limit_bytes=54 * 2**20),
         name="update",
     )(keeps, matrix, raw, high, low, stored)
 

time: 181 us -> 187 us (1.033)
  the two profiles are of different devices: /device:TPU:1 before, /device:TPU:6 now
where the time goes in v4:
time: 187 us; the launch traced here: 183 us
  starting transfers between devices  65.8 us (35%)
  blocking collectives  38.3 us (20%)
  waiting for transfers between devices  31.4 us (17%)
  Pallas kernels  17.1 us (9%)
  between operations  15.3 us (8%)
  local copies, waits for them, and re-layouts  12.8 us (7%)
  other arithmetic  2.17 us (1%)
    all_to_all x2, blocking collectives, exchange(): lax.all_to_all(pieces, axis, split_axis=0, concat_axis=0, tiled=True, axi...  38.3 us
    ppermute x15, starting transfers between devices, scatter_rows(): came[d] = lax.ppermute(came[d], ROWS, pairs)  29.9 us
    ppermute x15, waiting for transfers between devices, scatter_rows(): came[d] = lax.ppermute(came[d], ROWS, pairs)  27.3 us
    all_to_all x2, starting transfers between devices, exchange(): lax.all_to_all(pieces, axis, split_axis=0, concat_axis=0, tiled=True, axi...  13.1 us
    ppermute x3, starting transfers between devices, tree_copies(): came = lax.ppermute(own, ROWS, [(0, c), (1, c + 1)])  11.7 us
    ppermute x3, starting transfers between devices, tree_copies(): leaves.append(lax.ppermute(held, ROWS, pairs))  9.23 us
    pallas_call x1, Pallas kernels, update(): pl.pallas_call(functools.partial(update_kernel, steps, length), grid_spec...  8.71 us
    pallas_call x1, Pallas kernels, factors(): pl.pallas_call(functools.partial(factors_kernel, lines, lane, n_rows), in...  7.13 us
  transfers between devices with their start and end apart: 25, of which 11 were waited for; matrix products, arithmetic and copies ran while one was open for 4% of the time, Pallas kernels for 5%

profile of v4, /device:TPU:6, one launch (start us, length us, event | category | flops | bytes accessed | tf_op | source)
XLA Modules:
  0.0 182.9 jit_solution(5754679071739713770)
XLA Ops:
  9.0 9.6 %all-to-all-start = ((f32[32,16,512]{2,1,0:T(8,128)}), f32[32,16,512]{2,1,0:T(8,128)S(1)}, u32[]{:S(2)}, u32[]{:S(2)}) async-start(f32[32,16,512]{2,1,0:T(8,128)} %bitcast.15), calls=%async_computation | async-start | bytes 2097152 | tf_op jit(solution)/shard_map/all_to_all | solution.py:16
  18.7 1.5 slice-done
  20.2 2.0 %maximum_select_fusion = f32[512,1024]{1,0:T(8,128)S(1)} fusion(f32[512,1024]{1,0:T(8,128)} %matrix.1, f32[32,1024]{1,0:T(8,128)S(1)} %slice-done.1, f32[480,1024]{1,0:T(8,128)S(1)} %slice-done, pred[]{:T(512)S(6)} %eq.58), kind=kLoop, calls=%fused_computation.2 | loop fusion | flops 1048576 | bytes 6291457 | tf_op jit(solution)/shard_map/jit(_where)/select_n | solution.py:47
  22.4 1.3 collective-permute-start
  23.7 3.2 %collective-permute-start.1 = (f32[32,1024]{1,0:T(8,128)S(1)}, f32[32,1024]{1,0:T(8,128)S(1)}, u32[]{:S(2)}, u32[]{:S(2)}) collective-permute-start(f32[32,1024]{1,0:T(8,128)S(1)} %get-tuple-element.27), channel_id=1, source_target_pairs={{0,64},{32,96},{1,65},{33,97},{2,66},{34,98},{3,67},{35,99},{4,68}... | collective-permute-start | bytes 393224 | tf_op jit(solution)/shard_map/ppermute | solution.py:51
  27.0 9.3 %collective-permute-start.10 = (f32[32,1024]{1,0:T(8,128)S(1)}, f32[32,1024]{1,0:T(8,128)S(1)}, u32[]{:S(2)}, u32[]{:S(2)}) collective-permute-start(f32[32,1024]{1,0:T(8,128)S(1)} %get-tuple-element.18), channel_id=1, source_target_pairs={{0,352},{32,384},{1,353},{33,385},{2,354},{34,386},{3,355},{35,387... | collective-permute-start | bytes 393224 | tf_op jit(solution)/shard_map/ppermute | solution.py:51
  36.2 1.3 collective-permute-start.11
  37.5 1.3 collective-permute-start.12
  40.2 1.9 %collective-permute-start.14 = (f32[32,1024]{1,0:T(8,128)S(1)}, f32[32,1024]{1,0:T(8,128)S(1)}, u32[]{:S(2)}, u32[]{:S(2)}) collective-permute-start(f32[32,1024]{1,0:T(8,128)S(1)} %get-tuple-element.14), channel_id=1, source_target_pairs={{0,480},{32,0},{1,481},{33,1},{2,482},{34,2},{3,483},{35,3},{4,484... | collective-permute-start | bytes 393224 | tf_op jit(solution)/shard_map/ppermute | solution.py:51
  42.1 7.7 %collective-permute-done.10.refs_11_ = f32[32,1024]{1,0:T(8,128)S(1)} collective-permute-done((f32[32,1024]{1,0:T(8,128)S(1)}, f32[32,1024]{1,0:T(8,128)S(1)}, u32[]{:S(2)}, u32[]{:S(2)}) %collective-permute-start.10) | collective-permute-done | bytes 131104 | tf_op jit(solution)/shard_map/ppermute | solution.py:51
  51.1 7.1 %collective-permute-done.11.refs_12_ = f32[32,1024]{1,0:T(8,128)S(1)} collective-permute-done((f32[32,1024]{1,0:T(8,128)S(1)}, f32[32,1024]{1,0:T(8,128)S(1)}, u32[]{:S(2)}, u32[]{:S(2)}) %collective-permute-start.11) | collective-permute-done | bytes 131104 | tf_op jit(solution)/shard_map/ppermute | solution.py:51
  59.5 1.6 collective-permute-done.12.refs_13_
  62.3 1.5 collective-permute-done.13.refs_14_
  65.1 4.3 %collective-permute-done.14.refs_15_ = f32[32,1024]{1,0:T(8,128)S(1)} collective-permute-done((f32[32,1024]{1,0:T(8,128)S(1)}, f32[32,1024]{1,0:T(8,128)S(1)}, u32[]{:S(2)}, u32[]{:S(2)}) %collective-permute-start.14) | collective-permute-done | bytes 131104 | tf_op jit(solution)/shard_map/ppermute | solution.py:51
  72.0 1.3 collective-permute-start.8
  74.7 1.8 %collective-permute-done.7.refs_8_ = f32[32,1024]{1,0:T(8,128)S(1)} collective-permute-done((f32[32,1024]{1,0:T(8,128)S(1)}, f32[32,1024]{1,0:T(8,128)S(1)}, u32[]{:S(2)}, u32[]{:S(2)}) %collective-permute-start.7) | collective-permute-done | bytes 131104 | tf_op jit(solution)/shard_map/ppermute | solution.py:51
  76.5 1.4 collective-permute-done.8.refs_9_
  77.9 2.0 %collective-permute-done.9.refs_10_ = f32[32,1024]{1,0:T(8,128)S(1)} collective-permute-done((f32[32,1024]{1,0:T(8,128)S(1)}, f32[32,1024]{1,0:T(8,128)S(1)}, u32[]{:S(2)}, u32[]{:S(2)}) %collective-permute-start.9) | collective-permute-done | bytes 131104 | tf_op jit(solution)/shard_map/ppermute | solution.py:51
  82.5 9.1 %collective-permute-start.16 = (f32[16,512]{1,0:T(8,128)S(1)}, f32[16,512]{1,0:T(8,128)S(1)}, u32[]{:S(2)}, u32[]{:S(2)}) collective-permute-start(f32[16,512]{1,0:T(8,128)S(1)} %get-tuple-element.30), channel_id=1, source_target_pairs={{0,256},{32,288},{1,257},{33,289},{2,258},{34,290},{3,259},{35,291... | collective-permute-start | bytes 98312 | tf_op jit(solution)/shard_map/ppermute | solution.py:70
  93.6 3.5 %all-to-all-start.1 = ((f32[16,8,128]{2,1,0:T(8,128)}), f32[16,8,128]{2,1,0:T(8,128)S(1)}, u32[]{:S(2)}, u32[]{:S(2)}) async-start(f32[16,8,128]{2,1,0:T(8,128)} %broadcast_in_dim.15), calls=%async_computation.1 | async-start | bytes 131072 | tf_op jit(solution)/shard_map/all_to_all | solution.py:16
  97.2 5.0 %collective-permute-start.18 = (f32[16,512]{1,0:T(8,128)S(1)}, f32[16,512]{1,0:T(8,128)S(1)}, u32[]{:S(2)}, u32[]{:S(2)}) collective-permute-start(f32[16,512]{1,0:T(8,128)S(1)} %select_select_fusion), channel_id=1, source_target_pairs={{0,480},{32,0},{128,96},{160,128},{256,224},{288,256},{384,352},{4... | collective-permute-start | bytes 98312 | tf_op jit(solution)/shard_map/ppermute | solution.py:75
  103.5 3.0 %collective-permute-start.20 = (f32[16,512]{1,0:T(8,128)S(1)}, f32[16,512]{1,0:T(8,128)S(1)}, u32[]{:S(2)}, u32[]{:S(2)}) collective-permute-start(f32[16,512]{1,0:T(8,128)S(1)} %select_select_fusion), channel_id=1, source_target_pairs={{0,32},{32,64},{128,160},{160,192},{256,288},{288,320},{384,416},{... | collective-permute-start | bytes 98312 | tf_op jit(solution)/shard_map/ppermute | solution.py:75
  106.5 1.7 collective-permute-done.20
  108.2 1.8 all-to-all-done.1
  110.1 12.0 %all_to_all.20 = f32[4,96,512]{2,1,0:T(8,128)S(1)} all-to-all(f32[4,96,512]{2,1,0:T(8,128)S(1)} %broadcast_in_dim.16), channel_id=1, replica_groups={{0,8,16,24},{2,10,18,26},{4,12,20,28},{6,14,22,30},{1,3,5,7},{9,11,13,1..., dimensions={0} | all-to-all | bytes 1572864 | tf_op jit(solution)/shard_map/all_to_all | solution.py:16
  122.5 26.3 %all_to_all.21 = f32[4,4,96,512]{3,2,1,0:T(8,128)S(1)} all-to-all(f32[4,4,96,512]{3,2,1,0:T(8,128)S(1)} %broadcast_in_dim.17), channel_id=1, replica_groups={{0,2,4,6},{8,10,12,14},{16,18,20,22},{24,26,28,30},{1,9,17,25},{3,11,19..., dimensions={0} | all-to-all | bytes 6291456 | tf_op jit(solution)/shard_map/all_to_all | solution.py:16
  148.8 1.9 %collective-permute-start.21 = (f32[16,96,512]{2,1,0:T(8,128)S(1)}, f32[16,96,512]{2,1,0:T(8,128)}, u32[]{:S(2)}, u32[]{:S(2)}) collective-permute-start(f32[16,96,512]{2,1,0:T(8,128)S(1)} %bitcast.52), channel_id=1, source_target_pairs={{0,1},{1,0},{2,3},{3,2},{4,5},{5,4},{6,7},{7,6},{8,9},{9,8},{10,11... | collective-permute-start | bytes 9437192 | tf_op jit(solution)/shard_map/ppermute | solution.py:108
  154.6 1.3 concatenate.11.masks
  156.4 7.1 %factors.1 = (bf16[2,512,1024]{2,1,0:T(8,128)(2,1)S(1)}, bf16[2,512,1024]{2,1,0:T(8,128)(2,1)S(1)}, f32[512,512]{1,0:T(8,128)S(1)}) custom-call(s32[10]{0:T(128)S(1)} %concatenate.11.masks, f32[16,96,512]{2,1,0:T(8,128)S(1)} %bitcast.53, f32[16,96,512]{2,1,0:T(8,128)} %collective-permute-done.21.other), custom_call_target="tpu_custom_call" | custom-call | flops 4026531840 | bytes 6291456 | tf_op jit(solution)/shard_map/factors/pallas_call | solution.py:155
  163.6 1.4 copy-done
  165.0 1.4 copy-done.1
  167.3 8.7 %update.1 = f32[512,1024]{1,0:T(8,128)} custom-call(s32[1]{0:T(128)} %bitcast.keeps, f32[512,1024]{1,0:T(8,128)} %matrix.1, f32[1024,1024]{1,0:T(8,128)} %all-gather.2.cloned.1.call-done.raw, bf16[2,512,1024]{2,1,0:T(8,128)(2,1)} %copy-done, bf16[2,512,1024]{2,1,0:T(8,128)(2,1)} %copy-done.1, f32[512,512]{1,0:T(8,128)} %copy-done.2), custom_call_target="tpu_custom_call" | custom-call | flops 3221225472 | bytes 16777216 | tf_op jit(solution)/shard_map/update/pallas_call | solution.py:184
  (66 shorter events, 23.5 us)
Async XLA Ops:
  9.0 72.2 %all-to-all-start = ((f32[32,16,512]{2,1,0:T(8,128)}), f32[32,16,512]{2,1,0:T(8,128)S(1)}, u32[]{:S(2)}, u32[]{:S(2)}) async-start(f32[32,16,512]{2,1,0:T(8,128)} %bitcast.15), calls=%async_computation | async-start | bytes 2097152 | tf_op jit(solution)/shard_map/all_to_all | solution.py:16
  18.6 148.8 %all-gather.2.cloned.1.call-start = ((), (), s32[]{:S(2)}) async-start(), calls=%async_computation.4 | async-start | bytes 4456448 | tf_op jit(solution)/shard_map/all_gather | solution.py:219
  18.6 1.6 slice-start
  18.6 1.5 slice-start.1
  22.2 52.5 %copy-start.3 = (f32[2,32,512]{2,1,0:T(8,128)S(1)}, f32[2,32,512]{2,1,0:T(8,128)}, u32[]{:S(2)}) copy-start(f32[2,32,512]{2,1,0:T(8,128)} %param.7) | copy-start | bytes 393220
  22.4 16.4 %collective-permute-start = (f32[32,1024]{1,0:T(8,128)S(1)}, f32[32,1024]{1,0:T(8,128)S(1)}, u32[]{:S(2)}, u32[]{:S(2)}) collective-permute-start(f32[32,1024]{1,0:T(8,128)S(1)} %get-tuple-element.28), channel_id=1, source_target_pairs={{0,32},{32,64},{1,33},{33,65},{2,34},{34,66},{3,35},{35,67},{4,36}... | collective-permute-start | bytes 393224 | tf_op jit(solution)/shard_map/ppermute | solution.py:51
  23.7 16.4 %collective-permute-start.1 = (f32[32,1024]{1,0:T(8,128)S(1)}, f32[32,1024]{1,0:T(8,128)S(1)}, u32[]{:S(2)}, u32[]{:S(2)}) collective-permute-start(f32[32,1024]{1,0:T(8,128)S(1)} %get-tuple-element.27), channel_id=1, source_target_pairs={{0,64},{32,96},{1,65},{33,97},{2,66},{34,98},{3,67},{35,99},{4,68}... | collective-permute-start | bytes 393224 | tf_op jit(solution)/shard_map/ppermute | solution.py:51
  27.0 22.8 %collective-permute-start.10 = (f32[32,1024]{1,0:T(8,128)S(1)}, f32[32,1024]{1,0:T(8,128)S(1)}, u32[]{:S(2)}, u32[]{:S(2)}) collective-permute-start(f32[32,1024]{1,0:T(8,128)S(1)} %get-tuple-element.18), channel_id=1, source_target_pairs={{0,352},{32,384},{1,353},{33,385},{2,354},{34,386},{3,355},{35,387... | collective-permute-start | bytes 393224 | tf_op jit(solution)/shard_map/ppermute | solution.py:51
  36.2 22.0 %collective-permute-start.11 = (f32[32,1024]{1,0:T(8,128)S(1)}, f32[32,1024]{1,0:T(8,128)S(1)}, u32[]{:S(2)}, u32[]{:S(2)}) collective-permute-start(f32[32,1024]{1,0:T(8,128)S(1)} %get-tuple-element.17), channel_id=1, source_target_pairs={{0,384},{32,416},{1,385},{33,417},{2,386},{34,418},{3,387},{35,419... | collective-permute-start | bytes 393224 | tf_op jit(solution)/shard_map/ppermute | solution.py:51
  37.5 23.5 %collective-permute-start.12 = (f32[32,1024]{1,0:T(8,128)S(1)}, f32[32,1024]{1,0:T(8,128)S(1)}, u32[]{:S(2)}, u32[]{:S(2)}) collective-permute-start(f32[32,1024]{1,0:T(8,128)S(1)} %get-tuple-element.16), channel_id=1, source_target_pairs={{0,416},{32,448},{1,417},{33,449},{2,418},{34,450},{3,419},{35,451... | collective-permute-start | bytes 393224 | tf_op jit(solution)/shard_map/ppermute | solution.py:51
  38.8 25.0 %collective-permute-start.13 = (f32[32,1024]{1,0:T(8,128)S(1)}, f32[32,1024]{1,0:T(8,128)S(1)}, u32[]{:S(2)}, u32[]{:S(2)}) collective-permute-start(f32[32,1024]{1,0:T(8,128)S(1)} %get-tuple-element.15), channel_id=1, source_target_pairs={{0,448},{32,480},{1,449},{33,481},{2,450},{34,482},{3,451},{35,483... | collective-permute-start | bytes 393224 | tf_op jit(solution)/shard_map/ppermute | solution.py:51
  40.2 29.3 %collective-permute-start.14 = (f32[32,1024]{1,0:T(8,128)S(1)}, f32[32,1024]{1,0:T(8,128)S(1)}, u32[]{:S(2)}, u32[]{:S(2)}) collective-permute-start(f32[32,1024]{1,0:T(8,128)S(1)} %get-tuple-element.14), channel_id=1, source_target_pairs={{0,480},{32,0},{1,481},{33,1},{2,482},{34,2},{3,483},{35,3},{4,484... | collective-permute-start | bytes 393224 | tf_op jit(solution)/shard_map/ppermute | solution.py:51
  49.8 20.9 %collective-permute-start.2 = (f32[32,1024]{1,0:T(8,128)S(1)}, f32[32,1024]{1,0:T(8,128)S(1)}, u32[]{:S(2)}, u32[]{:S(2)}) collective-permute-start(f32[32,1024]{1,0:T(8,128)S(1)} %get-tuple-element.26), channel_id=1, source_target_pairs={{0,96},{32,128},{1,97},{33,129},{2,98},{34,130},{3,99},{35,131},{4... | collective-permute-start | bytes 393224 | tf_op jit(solution)/shard_map/ppermute | solution.py:51
  58.2 13.8 %collective-permute-start.3 = (f32[32,1024]{1,0:T(8,128)S(1)}, f32[32,1024]{1,0:T(8,128)S(1)}, u32[]{:S(2)}, u32[]{:S(2)}) collective-permute-start(f32[32,1024]{1,0:T(8,128)S(1)} %get-tuple-element.25), channel_id=1, source_target_pairs={{0,128},{32,160},{1,129},{33,161},{2,130},{34,162},{3,131},{35,163... | collective-permute-start | bytes 393224 | tf_op jit(solution)/shard_map/ppermute | solution.py:51
  61.0 12.3 %collective-permute-start.4 = (f32[32,1024]{1,0:T(8,128)S(1)}, f32[32,1024]{1,0:T(8,128)S(1)}, u32[]{:S(2)}, u32[]{:S(2)}) collective-permute-start(f32[32,1024]{1,0:T(8,128)S(1)} %get-tuple-element.24), channel_id=1, source_target_pairs={{0,160},{32,192},{1,161},{33,193},{2,162},{34,194},{3,163},{35,195... | collective-permute-start | bytes 393224 | tf_op jit(solution)/shard_map/ppermute | solution.py:51
  63.8 10.8 %collective-permute-start.5 = (f32[32,1024]{1,0:T(8,128)S(1)}, f32[32,1024]{1,0:T(8,128)S(1)}, u32[]{:S(2)}, u32[]{:S(2)}) collective-permute-start(f32[32,1024]{1,0:T(8,128)S(1)} %get-tuple-element.23), channel_id=1, source_target_pairs={{0,192},{32,224},{1,193},{33,225},{2,194},{34,226},{3,195},{35,227... | collective-permute-start | bytes 393224 | tf_op jit(solution)/shard_map/ppermute | solution.py:51
  69.4 5.3 %collective-permute-start.6 = (f32[32,1024]{1,0:T(8,128)S(1)}, f32[32,1024]{1,0:T(8,128)S(1)}, u32[]{:S(2)}, u32[]{:S(2)}) collective-permute-start(f32[32,1024]{1,0:T(8,128)S(1)} %get-tuple-element.22), channel_id=1, source_target_pairs={{0,224},{32,256},{1,225},{33,257},{2,226},{34,258},{3,227},{35,259... | collective-permute-start | bytes 393224 | tf_op jit(solution)/shard_map/ppermute | solution.py:51
  70.7 5.8 %collective-permute-start.7 = (f32[32,1024]{1,0:T(8,128)S(1)}, f32[32,1024]{1,0:T(8,128)S(1)}, u32[]{:S(2)}, u32[]{:S(2)}) collective-permute-start(f32[32,1024]{1,0:T(8,128)S(1)} %get-tuple-element.21), channel_id=1, source_target_pairs={{0,256},{32,288},{1,257},{33,289},{2,258},{34,290},{3,259},{35,291... | collective-permute-start | bytes 393224 | tf_op jit(solution)/shard_map/ppermute | solution.py:51
  72.0 5.9 %collective-permute-start.8 = (f32[32,1024]{1,0:T(8,128)S(1)}, f32[32,1024]{1,0:T(8,128)S(1)}, u32[]{:S(2)}, u32[]{:S(2)}) collective-permute-start(f32[32,1024]{1,0:T(8,128)S(1)} %get-tuple-element.20), channel_id=1, source_target_pairs={{0,288},{32,320},{1,289},{33,321},{2,290},{34,322},{3,291},{35,323... | collective-permute-start | bytes 393224 | tf_op jit(solution)/shard_map/ppermute | solution.py:51
  73.3 6.5 %collective-permute-start.9 = (f32[32,1024]{1,0:T(8,128)S(1)}, f32[32,1024]{1,0:T(8,128)S(1)}, u32[]{:S(2)}, u32[]{:S(2)}) collective-permute-start(f32[32,1024]{1,0:T(8,128)S(1)} %get-tuple-element.19), channel_id=1, source_target_pairs={{0,320},{32,352},{1,321},{33,353},{2,322},{34,354},{3,323},{35,355... | collective-permute-start | bytes 393224 | tf_op jit(solution)/shard_map/ppermute | solution.py:51
  81.2 15.9 %collective-permute-start.15 = (f32[16,512]{1,0:T(8,128)S(1)}, f32[16,512]{1,0:T(8,128)S(1)}, u32[]{:S(2)}, u32[]{:S(2)}) collective-permute-start(f32[16,512]{1,0:T(8,128)S(1)} %get-tuple-element.30), channel_id=1, source_target_pairs={{0,384},{32,416},{1,385},{33,417},{2,386},{34,418},{3,387},{35,419... | collective-permute-start | bytes 98312 | tf_op jit(solution)/shard_map/ppermute | solution.py:70
  82.5 14.6 %collective-permute-start.16 = (f32[16,512]{1,0:T(8,128)S(1)}, f32[16,512]{1,0:T(8,128)S(1)}, u32[]{:S(2)}, u32[]{:S(2)}) collective-permute-start(f32[16,512]{1,0:T(8,128)S(1)} %get-tuple-element.30), channel_id=1, source_target_pairs={{0,256},{32,288},{1,257},{33,289},{2,258},{34,290},{3,259},{35,291... | collective-permute-start | bytes 98312 | tf_op jit(solution)/shard_map/ppermute | solution.py:70
  91.6 5.5 %collective-permute-start.17 = (f32[16,512]{1,0:T(8,128)S(1)}, f32[16,512]{1,0:T(8,128)S(1)}, u32[]{:S(2)}, u32[]{:S(2)}) collective-permute-start(f32[16,512]{1,0:T(8,128)S(1)} %get-tuple-element.30), channel_id=1, source_target_pairs={{0,128},{32,160},{1,129},{33,161},{2,130},{34,162},{3,131},{35,163... | collective-permute-start | bytes 98312 | tf_op jit(solution)/shard_map/ppermute | solution.py:70
  93.6 16.4 %all-to-all-start.1 = ((f32[16,8,128]{2,1,0:T(8,128)}), f32[16,8,128]{2,1,0:T(8,128)S(1)}, u32[]{:S(2)}, u32[]{:S(2)}) async-start(f32[16,8,128]{2,1,0:T(8,128)} %broadcast_in_dim.15), calls=%async_computation.1 | async-start | bytes 131072 | tf_op jit(solution)/shard_map/all_to_all | solution.py:16
  97.2 9.3 %collective-permute-start.18 = (f32[16,512]{1,0:T(8,128)S(1)}, f32[16,512]{1,0:T(8,128)S(1)}, u32[]{:S(2)}, u32[]{:S(2)}) collective-permute-start(f32[16,512]{1,0:T(8,128)S(1)} %select_select_fusion), channel_id=1, source_target_pairs={{0,480},{32,0},{128,96},{160,128},{256,224},{288,256},{384,352},{4... | collective-permute-start | bytes 98312 | tf_op jit(solution)/shard_map/ppermute | solution.py:75
  102.2 4.3 %collective-permute-start.19 = (f32[16,512]{1,0:T(8,128)S(1)}, f32[16,512]{1,0:T(8,128)S(1)}, u32[]{:S(2)}, u32[]{:S(2)}) collective-permute-start(f32[16,512]{1,0:T(8,128)S(1)} %select_select_fusion), channel_id=1, source_target_pairs={{0,64},{32,96},{128,192},{160,224},{256,320},{288,352},{384,448},{... | collective-permute-start | bytes 98312 | tf_op jit(solution)/shard_map/ppermute | solution.py:75
  103.5 4.7 %collective-permute-start.20 = (f32[16,512]{1,0:T(8,128)S(1)}, f32[16,512]{1,0:T(8,128)S(1)}, u32[]{:S(2)}, u32[]{:S(2)}) collective-permute-start(f32[16,512]{1,0:T(8,128)S(1)} %select_select_fusion), channel_id=1, source_target_pairs={{0,32},{32,64},{128,160},{160,192},{256,288},{288,320},{384,416},{... | collective-permute-start | bytes 98312 | tf_op jit(solution)/shard_map/ppermute | solution.py:75
  122.4 28.3 %copy-start.5 = (s32[2,64]{1,0:T(2,128)S(1)}, s32[2,64]{1,0:T(2,128)}, u32[]{:S(2)}) copy-start(s32[2,64]{1,0:T(2,128)} %param.9) | copy-start | bytes 1540
  122.5 30.2 %copy-start.4 = (s32[2,16]{1,0:T(2,128)S(1)}, s32[2,16]{1,0:T(2,128)}, u32[]{:S(2)}) copy-start(s32[2,16]{1,0:T(2,128)} %param.8) | copy-start | bytes 388
  148.8 7.7 %collective-permute-start.21 = (f32[16,96,512]{2,1,0:T(8,128)S(1)}, f32[16,96,512]{2,1,0:T(8,128)}, u32[]{:S(2)}, u32[]{:S(2)}) collective-permute-start(f32[16,96,512]{2,1,0:T(8,128)S(1)} %bitcast.52), channel_id=1, source_target_pairs={{0,1},{1,0},{2,3},{3,2},{4,5},{5,4},{6,7},{7,6},{8,9},{9,8},{10,11... | collective-permute-start | bytes 9437192 | tf_op jit(solution)/shard_map/ppermute | solution.py:108
  163.6 1.4 copy-start
  165.0 1.4 copy-start.1
  (1 other events, 1.0 us)
Sparse Core Ops, SparseCore 0:
  81.3 80.6 all-gather.1
